TPU v7x, 512 devices: a whole 4x8x8 slice. The times are simulated.
512 devices in a mesh: seq: 64 (over z, x, core), chan: 8 (over y).
Axes of the slice: x: 4, y: 8, z: 8, core: 2. Of those that a mesh axis runs over, the one named last changes fastest.
Arguments:
- step_size: bfloat16 [2, 5120, 8192], P(None, ('chan', 'seq')), as said below
- inputs: bfloat16 [2, 5120, 8192], P(None, ('chan', 'seq')), may hold values from -6 to 6
- gate_input: bfloat16 [2, 5120, 8192], P(None, ('chan', 'seq')), may hold values from -6 to 6
- decay_rate: float32 [5120], P('chan'), as said below
- norm_gain: float32 [5120], P('chan'), may hold values from 0.1 to 1.9
- resets: int32 [2, 8], replicated, may hold values from 1 to 8191
Outputs:
- normed: bfloat16 [2, 5120, 8192], P(None, 'chan', 'seq')
Inputs may be any that keep to these rules, and one draw needn't show every extreme that they name: `step_size`: positive step sizes. `decay_rate`: positive rates. `resets`: positions within the sequence; several may coincide.
All inputs are finite; a program needn't handle non-finite values.
Results may differ from a plain program's by a relative error of at most 0.001.
Values may be sent and summed in bfloat16 or wider, within the bound.
No kernel may reach another device: no remote copies, remote signals or barrier semaphores. Data moves between devices by JAX's collectives and lax.ppermute only.
A program may use at most 64 MiB of HBM per device.

v0:
```python
import math

import jax
import jax.numpy as jnp
from jax import lax
from jax.sharding import Mesh
from jax.sharding import PartitionSpec as P

FEATURE_WIDTH = 5120
SEQ = ("seq_0", "seq_1", "seq_2")
CHAN_SEQ = ("chan", "seq_0", "seq_1", "seq_2")


def copy_for_each(array, axis):
    peers = lax.axis_size(axis)
    return lax.all_to_all(
        jnp.broadcast_to(array[None], (peers, *array.shape)), axis, 0, 0, tiled=True
    )


def taken_together(array, axis):
    return copy_for_each(array, axis).sum(axis=0)


def in_blocks(array, dim, peers):
    before, after = (array.shape[:dim], array.shape[dim + 1 :])
    return jnp.moveaxis(array.reshape(*before, peers, -1, *after), dim, 0)


def joined_along(blocks, dim):
    shape = list(blocks.shape[1:])
    shape[dim] *= blocks.shape[0]
    return jnp.moveaxis(blocks, 0, dim).reshape(shape)


def exchange_in_order(blocks, axes, sequence):
    inside = blocks.shape[1:]
    result = blocks.reshape(*(lax.axis_size(a) for a in axes), *inside)
    for k in sequence:
        result = lax.all_to_all(result, axes[k], k, k, tiled=True)
    return result.reshape(-1, *inside)


def core_and_chips(array, groups, sequence, split_dim, concat_dim):
    peers = lax.axis_size(groups[0]) * lax.axis_size(groups[1])
    blocks = in_blocks(array, split_dim, peers)
    return joined_along(exchange_in_order(blocks, groups, sequence), concat_dim)


def compose(earlier, later):
    return (earlier[0] * later[0], later[0] * earlier[1] + later[1])


def coefficients(steps, values, rates):
    scaled = steps.astype(jnp.float32) * rates[None, :, None]
    drive = jnp.sqrt(-jnp.expm1(-2.0 * scaled)) * values.astype(jnp.float32)
    return (scaled, drive)


def marks_for(resets, places):
    return jnp.any(resets[:, :, None] == places[None, None, :], axis=1)


def local_scan(scaled, drive, marks):
    rows, chans, length = scaled.shape
    places = jnp.arange(length, dtype=jnp.int32)
    upper = (places[:, None] <= places[None, :]).astype(jnp.float32)
    cumul = jnp.einsum("rck,ku->rcu", scaled, upper, precision=lax.Precision.HIGHEST)
    counts = jnp.dot(marks.astype(jnp.float32), upper, precision=lax.Precision.HIGHEST)
    linked = (counts[:, :, None] == counts[:, None, :]) & (places[:, None] >= places[None, :])[None]
    group = math.gcd(chans, 64)

    def one_group(pieces):
        cumul_part, drive_part = pieces
        spread = cumul_part[:, :, :, None] - cumul_part[:, :, None, :]
        weight = jnp.where(linked[:, None], jnp.exp(-jnp.maximum(spread, 0.0)), jnp.float32(0.0))
        return jnp.einsum("rctj,rcj->rct", weight, drive_part, precision=lax.Precision.HIGHEST)

    def split_groups(array):
        return jnp.moveaxis(array.reshape(rows, chans // group, group, length), 1, 0)

    results = lax.map(one_group, (split_groups(cumul), split_groups(drive)))
    local_state = jnp.moveaxis(results, 0, 1).reshape(rows, chans, length)
    running = jnp.where(counts[:, None, :] == 0.0, jnp.exp(-cumul), jnp.float32(0.0))
    return (running, local_state)


def finish(gated, norm_gain):
    squares = jnp.sum(gated * gated, axis=1)
    total = taken_together(squares, "chan")
    mean_square = total / jnp.float32(FEATURE_WIDTH)
    scale_rows = lax.rsqrt(mean_square + 1e-05)
    return (gated * scale_rows[:, None, :] * norm_gain[None, :, None]).astype(jnp.bfloat16)


def per_device(step_size, inputs, gate_input, decay_rate, norm_gain, resets):
    position = lax.axis_index(SEQ)
    batch, width, length = step_size.shape
    rates = lax.dynamic_slice_in_dim(decay_rate, position * width, width)
    places = jnp.arange(length, dtype=jnp.int32)
    scaled, drive = coefficients(step_size, inputs, rates)
    marks = marks_for(resets, places)
    piece = math.gcd(length, 128)
    count_blocks = length // piece

    def to_blocks(array):
        moved = jnp.moveaxis(array.reshape(batch, width, count_blocks, piece), 2, 1)
        return moved.reshape(batch * count_blocks, width, piece)

    running, local_state = local_scan(
        to_blocks(scaled), to_blocks(drive), marks.reshape(batch * count_blocks, piece)
    )
    total_decay = running[:, :, -1].reshape(batch, count_blocks, width)
    total_state = local_state[:, :, -1].reshape(batch, count_blocks, width)
    prefix = lax.associative_scan(compose, (total_decay, total_state), axis=1)
    incoming = jnp.concatenate(
        [jnp.zeros((batch, 1, width), jnp.float32), prefix[1][:, :-1]], axis=1
    )
    blocked = local_state + running * incoming.reshape(batch * count_blocks, width)[:, :, None]
    state = jnp.moveaxis(blocked.reshape(batch, count_blocks, width, piece), 1, 2).reshape(
        batch, width, length
    )
    local_gated = state * jax.nn.silu(gate_input.astype(jnp.float32))
    gated = core_and_chips(local_gated, (("seq_0", "seq_1"), "seq_2"), (0, 1), 2, 1)
    return finish(gated, norm_gain)


def solution(mesh):
    split = Mesh(
        mesh.devices.reshape(8, 4, 2, mesh.shape["chan"]), ("seq_0", "seq_1", "seq_2", "chan")
    )
    in_specs = (
        P(None, CHAN_SEQ, None),
        P(None, CHAN_SEQ, None),
        P(None, CHAN_SEQ, None),
        P("chan"),
        P("chan"),
        P(),
    )
    out_specs = P(None, "chan", SEQ)
    return jax.shard_map(
        per_device, mesh=split, in_specs=in_specs, out_specs=out_specs, check_vma=False
    )
```

profile of v0, /device:TPU:1, one launch (start us, length us, event | category | flops | bytes accessed | tf_op | source)
XLA Modules:
  0.0 248.5 jit_solution(6735893164475072453)
XLA Ops:
  0.0 0.8 dynamic_slice.10
  0.8 2.9 %convert_multiply_fusion.1 = (f32[2,10,8192]{2,0,1:T(2,128)S(1)}, f32[2,10,8192]{2,0,1:T(2,128)S(1)}) fusion(bf16[2,10,8192]{2,0,1:T(2,128)(2,1)} %param.9, f32[10]{0:T(128)S(1)} %dynamic_slice.10, bf16[2,10,8192]{2,0,1:T(2,128)(2,1)} %param.8), kind=kLoop, calls=%fused_computation.30 | loop fusion | flops 983040 | bytes 1966120 | tf_op jit(solution)/shard_map/mul | solution.py:56
  3.7 0.6 reshape.68
  4.3 0.3 fusion.18
  4.6 0.1 broadcast_compare_fusion
  4.8 0.4 exponential_select_fusion
  5.3 0.5 copy.94
  5.8 0.6 reshape.71
  6.3 168.6 %while.11 = (s32[]{:T(128)}, f32[5,128,2,128]{3,2,1,0:T(2,128)S(1)}, f32[5,128,2,128]{3,2,1,0:T(2,128)S(1)}, f32[5,128,2,128]{3,1,2,0:T(8,128)S(1)}, f32[128,128...) while((s32[]{:T(128)}, f32[5,128,2,128]{3,2,1,0:T(2,128)S(1)}, ...), condition=%wide.region_2.3_spmd.clone, body=%wide.region_1.2_spmd.clone.sunk | while | flops 71303168 | bytes 5718105 | solution.py:82
  6.7 5.3 %compare_and_fusion.2 = pred[128,128,128]{2,1,0:T(8,128)(4,1)S(1)} fusion(f32[128,128]{1,0:T(8,128)S(1)} %get-tuple-element.176, pred[128,128]{1,0:T(8,128)(4,1)S(1)} %get-tuple-element.177), kind=kLoop, calls=%fused_computation.10.clone.1 | loop fusion | flops 4194304 | bytes 2179072 | tf_op jit(solution)/shard_map/and | solution.py:70
  12.0 28.1 %fusion.41 = f32[128,2,1,128]{3,2,1,0:T(1,128)S(1)} fusion(f32[128,2,128,1]{2,3,1,0:T(1,128)S(1)} %bitcast.79, f32[128,2,128]{2,1,0:T(2,128)S(1)} %dynamic-slice_bitcast_fusion.2, pred[128,128,128]{2,1,0:T(8,128)(4,1)S(1)} %compare_and_fusion.2), kind=kOutput, calls=%fused_computation.1.clone.1 | convolution fusion | flops 67108864 | bytes 2490368 | tf_op jit(solution)/shard_map/while/body/eval_jaxpr/rctj,rcj->rct/dot_general | solution.py:77
  40.3 5.3 %compare_and_fusion.2 = pred[128,128,128]{2,1,0:T(8,128)(4,1)S(1)} fusion(f32[128,128]{1,0:T(8,128)S(1)} %get-tuple-element.176, pred[128,128]{1,0:T(8,128)(4,1)S(1)} %get-tuple-element.177), kind=kLoop, calls=%fused_computation.10.clone.1 | loop fusion | flops 4194304 | bytes 2179072 | tf_op jit(solution)/shard_map/and | solution.py:70
  45.7 28.1 %fusion.41 = f32[128,2,1,128]{3,2,1,0:T(1,128)S(1)} fusion(f32[128,2,128,1]{2,3,1,0:T(1,128)S(1)} %bitcast.79, f32[128,2,128]{2,1,0:T(2,128)S(1)} %dynamic-slice_bitcast_fusion.2, pred[128,128,128]{2,1,0:T(8,128)(4,1)S(1)} %compare_and_fusion.2), kind=kOutput, calls=%fused_computation.1.clone.1 | convolution fusion | flops 67108864 | bytes 2490368 | tf_op jit(solution)/shard_map/while/body/eval_jaxpr/rctj,rcj->rct/dot_general | solution.py:77
  74.0 5.3 %compare_and_fusion.2 = pred[128,128,128]{2,1,0:T(8,128)(4,1)S(1)} fusion(f32[128,128]{1,0:T(8,128)S(1)} %get-tuple-element.176, pred[128,128]{1,0:T(8,128)(4,1)S(1)} %get-tuple-element.177), kind=kLoop, calls=%fused_computation.10.clone.1 | loop fusion | flops 4194304 | bytes 2179072 | tf_op jit(solution)/shard_map/and | solution.py:70
  79.3 28.1 %fusion.41 = f32[128,2,1,128]{3,2,1,0:T(1,128)S(1)} fusion(f32[128,2,128,1]{2,3,1,0:T(1,128)S(1)} %bitcast.79, f32[128,2,128]{2,1,0:T(2,128)S(1)} %dynamic-slice_bitcast_fusion.2, pred[128,128,128]{2,1,0:T(8,128)(4,1)S(1)} %compare_and_fusion.2), kind=kOutput, calls=%fused_computation.1.clone.1 | convolution fusion | flops 67108864 | bytes 2490368 | tf_op jit(solution)/shard_map/while/body/eval_jaxpr/rctj,rcj->rct/dot_general | solution.py:77
  107.6 5.3 %compare_and_fusion.2 = pred[128,128,128]{2,1,0:T(8,128)(4,1)S(1)} fusion(f32[128,128]{1,0:T(8,128)S(1)} %get-tuple-element.176, pred[128,128]{1,0:T(8,128)(4,1)S(1)} %get-tuple-element.177), kind=kLoop, calls=%fused_computation.10.clone.1 | loop fusion | flops 4194304 | bytes 2179072 | tf_op jit(solution)/shard_map/and | solution.py:70
  112.9 28.1 %fusion.41 = f32[128,2,1,128]{3,2,1,0:T(1,128)S(1)} fusion(f32[128,2,128,1]{2,3,1,0:T(1,128)S(1)} %bitcast.79, f32[128,2,128]{2,1,0:T(2,128)S(1)} %dynamic-slice_bitcast_fusion.2, pred[128,128,128]{2,1,0:T(8,128)(4,1)S(1)} %compare_and_fusion.2), kind=kOutput, calls=%fused_computation.1.clone.1 | convolution fusion | flops 67108864 | bytes 2490368 | tf_op jit(solution)/shard_map/while/body/eval_jaxpr/rctj,rcj->rct/dot_general | solution.py:77
  141.2 5.3 %compare_and_fusion.2 = pred[128,128,128]{2,1,0:T(8,128)(4,1)S(1)} fusion(f32[128,128]{1,0:T(8,128)S(1)} %get-tuple-element.176, pred[128,128]{1,0:T(8,128)(4,1)S(1)} %get-tuple-element.177), kind=kLoop, calls=%fused_computation.10.clone.1 | loop fusion | flops 4194304 | bytes 2179072 | tf_op jit(solution)/shard_map/and | solution.py:70
  146.6 28.1 %fusion.41 = f32[128,2,1,128]{3,2,1,0:T(1,128)S(1)} fusion(f32[128,2,128,1]{2,3,1,0:T(1,128)S(1)} %bitcast.79, f32[128,2,128]{2,1,0:T(2,128)S(1)} %dynamic-slice_bitcast_fusion.2, pred[128,128,128]{2,1,0:T(8,128)(4,1)S(1)} %compare_and_fusion.2), kind=kOutput, calls=%fused_computation.1.clone.1 | convolution fusion | flops 67108864 | bytes 2490368 | tf_op jit(solution)/shard_map/while/body/eval_jaxpr/rctj,rcj->rct/dot_general | solution.py:77
  175.0 0.4 slice_reduce_fusion.1
  175.5 0.2 slice.149
  175.7 0.2 slice.150
  175.9 0.4 slice_reduce_fusion
  176.4 0.2 slice.148
  176.6 0.2 slice.152
  176.8 0.1 slice.155
  177.0 0.1 slice.156
  177.1 0.1 slice.154
  177.2 0.1 slice.158
  177.4 0.1 slice.161
  177.5 0.1 slice.162
  177.6 0.1 slice.160
  177.8 0.1 slice.164
  179.3 0.1 slice.159
  179.4 0.1 slice.184
  179.5 0.1 slice.153
  179.6 0.1 slice.186
  179.8 0.2 slice.188
  180.0 0.2 slice.147
  180.2 0.8 pad.41
  181.1 0.8 pad.40
  182.0 0.8 pad.42
  182.8 0.8 pad.43
  183.7 0.9 pad.45
  184.7 0.9 pad.44
  185.6 1.0 pad.46
  186.6 1.0 pad.47
  187.6 1.1 pad.77
  188.8 1.1 pad.61
  190.1 0.2 multiply_add_fusion
  190.4 0.4 reshape.74
  190.8 0.7 fusion.13
  191.5 0.6 reshape.75
  192.0 0.2 copy.81
  192.3 32.2 %all_to_all.15 = f32[32,2,2,10,128]{4,1,3,2,0:T(2,128)S(1)} all-to-all(f32[32,2,2,10,128]{4,1,3,2,0:T(2,128)S(1)} %copy.81), channel_id=1, replica_groups=mesh['seq_0'=8,'seq_1'=4,'seq_2'=2,'chan'=8] {'seq_0','seq_1'}, dimensions={0} | all-to-all | bytes 1310720 | tf_op jit(solution)/shard_map/all_to_all | solution.py:40
  224.5 0.3 copy.82
  224.8 6.4 %all_to_all.16 = f32[32,2,2,10,128]{4,2,3,0,1:T(2,128)S(1)} all-to-all(f32[32,2,2,10,128]{4,2,3,0,1:T(2,128)S(1)} %copy.82), channel_id=1, replica_groups=mesh['seq_0'=8,'seq_1'=4,'seq_2'=2,'chan'=8] {'seq_2'}, dimensions={1} | all-to-all | bytes 1310720 | tf_op jit(solution)/shard_map/all_to_all | solution.py:40
  231.2 0.5 copy.83
  231.8 0.6 broadcast_in_dim.36
  232.4 6.8 %all-to-all-start.2 = ((f32[8,2,128]{2,1,0:T(2,128)}), f32[8,2,128]{2,1,0:T(2,128)S(1)}, u32[]{:S(2)}, u32[]{:S(2)}) async-start(f32[8,2,128]{2,1,0:T(2,128)} %broadcast_in_dim.36), calls=%async_computation.2 | async-start | bytes 16384 | tf_op jit(solution)/shard_map/all_to_all | solution.py:16
  239.2 0.5 copy.84
  239.7 6.1 %all-to-all-done.2 = f32[8,2,128]{2,1,0:T(2,128)S(1)} async-done(((f32[8,2,128]{2,1,0:T(2,128)}), f32[8,2,128]{2,1,0:T(2,128)S(1)}, u32[]{:S(2)}, u32[]{:S(2)}) %all-to-all-start.2) | async-done | bytes 8224 | tf_op jit(solution)/shard_map/all_to_all | solution.py:16
  245.8 1.9 fusion.17
  247.7 0.8 copy.86
  (69 shorter events, 3.3 us)
Async XLA Ops:
  0.0 4.3 %copy-start.2 = (s32[2,8]{1,0:T(2,128)S(1)}, s32[2,8]{1,0:T(2,128)}, u32[]{:S(2)}) copy-start(s32[2,8]{1,0:T(2,128)} %param.13) | copy-start | bytes 196
  179.1 11.6 %copy-start = (bf16[2,10,8192]{2,0,1:T(2,128)(2,1)S(1)}, bf16[2,10,8192]{2,0,1:T(2,128)(2,1)}, u32[]{:S(2)}) copy-start(bf16[2,10,8192]{2,0,1:T(2,128)(2,1)} %param.10) | copy-start | bytes 983044
  224.8 21.0 %copy-start.1 = (f32[640]{0:T(1024)S(1)}, f32[640]{0:T(1024)}, u32[]{:S(2)}) copy-start(f32[640]{0:T(1024)} %param.12) | copy-start | bytes 7684
  232.4 13.4 %all-to-all-start.2 = ((f32[8,2,128]{2,1,0:T(2,128)}), f32[8,2,128]{2,1,0:T(2,128)S(1)}, u32[]{:S(2)}, u32[]{:S(2)}) async-start(f32[8,2,128]{2,1,0:T(2,128)} %broadcast_in_dim.36), calls=%async_computation.2 | async-start | bytes 16384 | tf_op jit(solution)/shard_map/all_to_all | solution.py:16
where the time goes:
time: 249 us; the launch traced here: 248 us
  matrix products  141 us (57%)
  blocking collectives  38.5 us (15%)
  other arithmetic  33.7 us (14%)
  local copies, waits for them, and re-layouts  21.3 us (9%)
  starting transfers between devices  6.84 us (3%)
  waiting for transfers between devices  6.07 us (2%)
    dot_general x5, matrix products, one_group(): jnp.einsum('rctj,rcj->rct', weight, drive_part, precision=lax.Precision.H...  140 us
    all_to_all x2, blocking collectives, exchange_in_order(): result = lax.all_to_all(result, axes[k], k, k, tiled=True)  38.5 us
    and x5, other arithmetic, local_scan(): (counts[:, :, None] == counts[:, None, :]) & (places[:, None] >= places[N...  26.7 us
    pad x8, local copies, waits for them, and re-layouts, per_device(): prefix = lax.associative_scan(compose, (total_decay, total_state), axis=1)  6.92 us
    all_to_all x1, starting transfers between devices, copy_for_each(): lax.all_to_all(jnp.broadcast_to(array[None], (peers, *array.shape)), axis...  6.84 us
    all_to_all x1, waiting for transfers between devices, copy_for_each(): lax.all_to_all(jnp.broadcast_to(array[None], (peers, *array.shape)), axis...  6.07 us
  transfers between devices with their start and end apart: 1, of which 1 were waited for; matrix products, arithmetic and copies ran while one was open for 0% of the time, Pallas kernels for 0%

commit v1 on v0

v1 whole, which is shorter than its diff:
```python
import functools
import math

import jax
import jax.numpy as jnp
from jax import lax
from jax.experimental import pallas as pl
from jax.experimental.pallas import tpu as pltpu
from jax.sharding import Mesh
from jax.sharding import PartitionSpec as P

FEATURE_WIDTH = 5120
SEQ = ("seq_0", "seq_1", "seq_2")
CHAN_SEQ = ("chan", "seq_0", "seq_1", "seq_2")
LANES = 128
SUB = 8
LEVELS = 32700.0
MIDDLE = 32768.0
FINE = 64.0
CODE_ZERO = 16384.0
LOG2E = 1.4426950408889634


def one_minus_exp(x, expo):
    t = jnp.minimum(x, 0.5)
    p = jnp.float32(-1.0 / 5040.0)
    p = p * t + jnp.float32(1.0 / 720.0)
    p = 1.0 / 120.0 - p * t
    p = 1.0 / 24.0 - p * t
    p = 1.0 / 6.0 - p * t
    p = 0.5 - p * t
    p = 1.0 - p * t
    return jnp.where(x < 0.5, t * p, 1.0 - expo * expo)


def rolled(x, k):
    return pltpu.roll(x, k, 1)


def scan_kernel(sizes, rate_ref, reset_ref, step_ref, inp_ref, gate_ref, out_ref, xs, marks, tot):
    batch, width, blocks, pitch, ndoc = sizes
    place = lax.axis_index(SEQ)
    groups = blocks // SUB
    rows = batch * width
    lane = lax.broadcasted_iota(jnp.int32, (SUB, LANES), 1)
    sub = lax.broadcasted_iota(jnp.int32, (SUB, LANES), 0)

    def bring(j, _):
        for k, ref in enumerate((step_ref, inp_ref, gate_ref)):
            for b in range(batch):
                for low in range(0, width, SUB):
                    n = min(SUB, width - low)
                    v = ref[b, low : low + n, pl.ds(pl.multiple_of(j * LANES, LANES), LANES)]
                    xs[k, pl.ds((b * width + low) * pitch + j, n, stride=pitch), :] = v.astype(
                        jnp.float32
                    )
        return 0

    lax.fori_loop(0, blocks, bring, 0, unroll=4)

    rate = [rate_ref[place * width + c] for c in range(width)]

    def local(m, _):
        first = m * SUB
        t = (first + sub) * LANES + lane
        ta = jnp.ones((SUB, LANES), jnp.float32)
        tb = jnp.zeros((SUB, LANES), jnp.float32)
        for b in range(batch):
            hit = t == reset_ref[b, 0]
            for k in range(1, ndoc):
                hit = hit | (t == reset_ref[b, k])
            for c in range(width):
                r = b * width + c
                at = pl.ds(r * pitch + first, SUB)
                scaled = xs[0, at, :] * rate[c]
                expo = jnp.exp2(scaled * (-LOG2E))
                drive = jnp.sqrt(one_minus_exp(scaled + scaled, expo)) * xs[1, at, :]
                a = jnp.where(hit, 0.0, expo)
                s = drive
                k = 1
                while k < LANES:
                    keep = lane >= k
                    s = s + a * jnp.where(keep, rolled(s, k), 0.0)
                    a = a * jnp.where(keep, rolled(a, k), 1.0)
                    k *= 2
                xs[0, at, :] = a
                xs[1, at, :] = s
                ta = jnp.where(lane == r, a[:, LANES - 1 :], ta)
                tb = jnp.where(lane == r, s[:, LANES - 1 :], tb)
        here = pl.ds(pl.multiple_of(first, SUB), SUB)
        tot[0, here, :] = ta
        tot[1, here, :] = tb
        return 0

    lax.fori_loop(0, groups, local, 0, unroll=2)

    carry = jnp.zeros((SUB, LANES), jnp.float32)
    for m in range(groups):
        ta = tot[0, m * SUB : (m + 1) * SUB, :]
        tb = tot[1, m * SUB : (m + 1) * SUB, :]
        for k in (1, 2, 4):
            keep = sub >= k
            tb = tb + ta * jnp.where(keep, pltpu.roll(tb, k, 0), 0.0)
            ta = ta * jnp.where(keep, pltpu.roll(ta, k, 0), 1.0)
        full = tb + ta * carry
        tot[0, m * SUB : (m + 1) * SUB, :] = jnp.where(sub == 0, carry, pltpu.roll(full, 1, 0))
        carry = jnp.broadcast_to(full[SUB - 1 :, :], (SUB, LANES))

    def emit(m, _):
        first = m * SUB
        start = tot[0, pl.ds(pl.multiple_of(first, SUB), SUB), :]
        packed = []
        code = None
        for b in range(batch):
            values = []
            top = jnp.full((SUB, LANES), 1e-37, jnp.float32)
            for c in range(width):
                r = b * width + c
                at = pl.ds(r * pitch + first, SUB)
                state = xs[1, at, :] + xs[0, at, :] * start[:, r : r + 1]
                g = xs[2, at, :]
                value = state * (g / (1.0 + jnp.exp2(g * (-LOG2E))))
                values.append(value)
                top = jnp.maximum(top, jnp.abs(value))
            e = jnp.ceil(jnp.log2(top) * FINE)
            inv = jnp.exp2(e * (-1.0 / FINE)) * LEVELS
            whole = [(v * inv + (MIDDLE + 0.5)).astype(jnp.int32) for v in values]
            whole.append((e + CODE_ZERO).astype(jnp.int32))
            packed.append(whole)
        for c in range(width + 1):
            word = packed[0][c] * 65536 | packed[1][c]
            out_ref[pl.ds(first * (width + 1) + c, SUB, stride=width + 1), :] = word
        return 0

    lax.fori_loop(0, groups, emit, 0)


def opened(word):
    return (
        lax.shift_right_logical(word, 16).astype(jnp.float32),
        (word & 65535).astype(jnp.float32),
    )


def scales(word):
    return [jnp.exp2((e - CODE_ZERO) * (1.0 / FINE)) * (1.0 / LEVELS) for e in opened(word)]


def squares_kernel(sizes, got_ref, sum_ref, keep_ref, send_ref):
    width, chips, cores, chan = sizes
    mine = lax.axis_index("seq_2")
    record = width + 1
    acc = [[None, None], [None, None]]
    for m in range(chips // SUB):
        base = m * SUB * cores * record
        codes = [
            got_ref[pl.ds(base + k * record + width, SUB, stride=cores * record), :]
            for k in range(cores)
        ]
        scale = [scales(w) for w in codes]
        for c in range(record):
            words = [
                got_ref[pl.ds(base + k * record + c, SUB, stride=cores * record), :]
                for k in range(cores)
            ]
            to = pl.ds(m * SUB * record + c, SUB, stride=record)
            keep_ref[to, :] = jnp.where(mine == 0, words[0], words[1])
            send_ref[to, :] = jnp.where(mine == 0, words[1], words[0])
            if c < width:
                for k in range(cores):
                    for b, q in enumerate(opened(words[k])):
                        v = (q - MIDDLE) * scale[k][b]
                        acc[k][b] = v * v if acc[k][b] is None else acc[k][b] + v * v
    for k in range(cores):
        for b in range(2):
            row = jnp.sum(acc[k][b], axis=0, keepdims=True)
            for y in range(chan):
                sum_ref[k * chan + y, b : b + 1, :] = row


def final_kernel(sizes, keep_ref, got_ref, sum_ref, gain_ref, out_ref, flat):
    width, chips, cores, peers = sizes
    mine = lax.axis_index("seq_2")
    record = width + 1
    total = sum_ref[0]
    for k in range(1, peers):
        total = total + sum_ref[k]
    norm = lax.rsqrt(total / jnp.float32(FEATURE_WIDTH) + 1e-5)
    for m in range(chips // SUB):
        def words(c):
            at = pl.ds(m * SUB * record + c, SUB, stride=record)
            a, b = keep_ref[at, :], got_ref[at, :]
            return jnp.where(mine == 0, a, b), jnp.where(mine == 0, b, a)

        scale = [scales(w) for w in words(width)]
        scale = [[s * norm[b : b + 1] for b, s in enumerate(pair)] for pair in scale]
        for c in range(width):
            for k, word in enumerate(words(c)):
                for b, q in enumerate(opened(word)):
                    row = m * SUB * cores * width + k * width + c
                    flat[b, pl.ds(row, SUB, stride=cores * width), :] = (q - MIDDLE) * scale[k][b]
    channels = out_ref.shape[1]
    for g in range(channels // LANES):
        gain = jnp.broadcast_to(gain_ref[g : g + 1, :], (LANES, LANES)).T
        for b in range(2):
            rows = slice(g * LANES, (g + 1) * LANES)
            out_ref[b, rows, :] = (flat[b, rows, :] * gain).astype(jnp.bfloat16)


def whole(space=pltpu.VMEM):
    return pl.BlockSpec(memory_space=space)


def per_device(step_size, inputs, gate_input, decay_rate, norm_gain, resets):
    batch, width, length = step_size.shape
    chips = lax.axis_size("seq_0") * lax.axis_size("seq_1")
    cores = lax.axis_size("seq_2")
    chan = lax.axis_size("chan")
    blocks = chips * cores
    record = width + 1
    pitch = blocks
    rows = batch * width
    words = pl.pallas_call(
        functools.partial(scan_kernel, (batch, width, blocks, pitch, resets.shape[1])),
        out_shape=jax.ShapeDtypeStruct((blocks * record, LANES), jnp.int32),
        in_specs=[whole(pltpu.SMEM), whole(pltpu.SMEM), whole(), whole(), whole()],
        out_specs=whole(),
        scratch_shapes=[
            pltpu.VMEM((3, rows * pitch, LANES), jnp.float32),
            pltpu.VMEM((batch, blocks, LANES), jnp.float32),
            pltpu.VMEM((2, blocks, LANES), jnp.float32),
        ],
        name="scan",
    )(decay_rate, resets, step_size, inputs, gate_input)
    words = words.reshape(chips, cores * record, 1, LANES)
    words = lax.all_to_all(words, ("seq_0", "seq_1"), 0, 0, tiled=True)
    words = words.reshape(chips * cores * record, LANES)
    half = jax.ShapeDtypeStruct((chips * record, LANES), jnp.int32)
    sums, keep, send = pl.pallas_call(
        functools.partial(squares_kernel, (width, chips, cores, chan)),
        out_shape=(jax.ShapeDtypeStruct((cores * chan, batch, LANES), jnp.float32), half, half),
        in_specs=[whole()],
        out_specs=(whole(), whole(), whole()),
        name="squares",
    )(words)
    sums = lax.all_to_all(sums, ("seq_2", "chan"), 0, 0, tiled=True)
    got = lax.ppermute(send, "seq_2", [(0, 1), (1, 0)])
    channels = chips * cores * width
    return pl.pallas_call(
        functools.partial(final_kernel, (width, chips, cores, cores * chan)),
        out_shape=jax.ShapeDtypeStruct((batch, channels, LANES), jnp.bfloat16),
        in_specs=[whole()] * 4,
        out_specs=whole(),
        scratch_shapes=[pltpu.VMEM((batch, channels, LANES), jnp.float32)],
        name="final",
    )(keep, got, sums, norm_gain.reshape(channels // LANES, LANES))


def solution(mesh):
    split = Mesh(
        mesh.devices.reshape(8, 4, 2, mesh.shape["chan"]), ("seq_0", "seq_1", "seq_2", "chan")
    )
    in_specs = (
        P(None, CHAN_SEQ, None),
        P(None, CHAN_SEQ, None),
        P(None, CHAN_SEQ, None),
        P("chan"),
        P("chan"),
        P(),
    )
    out_specs = P(None, "chan", SEQ)
    return jax.shard_map(
        per_device, mesh=split, in_specs=in_specs, out_specs=out_specs, check_vma=False
    )
```

time: 249 us -> 66.5 us (0.27)
  matrix products: 141 us -> 0 us
  other arithmetic: 33.7 us -> 0 us
  local copies, waits for them, and re-layouts: 21.3 us -> 4.68 us
  Pallas kernels: 0 us -> 15.8 us
  waiting for transfers between devices: 6.07 us -> 0.01 us
  blocking collectives: 38.5 us -> 41.5 us
  starting transfers between devices: 6.84 us -> 4.11 us
    dot_general x7 -> x0, matrix products: 141 us -> none  [the longest x5 140 us: one_group(): jnp.einsum('rctj,rcj->rct', weight, drive_part, precision=lax.Precision.H...]
    and x5 -> x0, other arithmetic: 26.7 us -> none  [local_scan(): (counts[:, :, None] == counts[:, None, :]) & (places[:, None] >= places[N...]
    pallas_call x0 -> x3, Pallas kernels: none -> 15.8 us  [the longest x1 12 us: per_device(): pl.pallas_call(functools.partial(scan_kernel, (batch, width, blocks, pitc...]
    pad x8 -> x0, local copies, waits for them, and re-layouts: 6.92 us -> none  [per_device(): prefix = lax.associative_scan(compose, (total_decay, total_state), axis=1)]
    all_to_all x1 -> x0, starting transfers between devices: 6.84 us -> none  [copy_for_each(): lax.all_to_all(jnp.broadcast_to(array[None], (peers, *array.shape)), axis...]
    all_to_all x1 -> x0, waiting for transfers between devices: 6.07 us -> none  [copy_for_each(): lax.all_to_all(jnp.broadcast_to(array[None], (peers, *array.shape)), axis...]
    slice x31 -> x0, local copies, waits for them, and re-layouts: 5.66 us -> none  [the longest x28 3.66 us: per_device(): prefix = lax.associative_scan(compose, (total_decay, total_state), axis=1)]
    ppermute x0 -> x1, starting transfers between devices: none -> 4.11 us  [per_device(): got = lax.ppermute(send, 'seq_2', [(0, 1), (1, 0)])]
  transfers between devices with their start and end apart: 1 -> 1, of which waited for: 1 -> 0; matrix products, arithmetic and copies ran while one was open for 0% -> 0% of each run, Pallas kernels for 0% -> 0%
where the time goes in v1:
time: 66.5 us; the launch traced here: 66.1 us
  blocking collectives  41.5 us (62%)
  Pallas kernels  15.8 us (24%)
  local copies, waits for them, and re-layouts  4.68 us (7%)
  starting transfers between devices  4.11 us (6%)
    all_to_all x1, blocking collectives, per_device(): words = lax.all_to_all(words, ('seq_0', 'seq_1'), 0, 0, tiled=True)  27.2 us
    all_to_all x1, blocking collectives, per_device(): sums = lax.all_to_all(sums, ('seq_2', 'chan'), 0, 0, tiled=True)  14.3 us
    pallas_call x1, Pallas kernels, per_device(): pl.pallas_call(functools.partial(scan_kernel, (batch, width, blocks, pitc...  12 us
    unnamed x9, local copies, waits for them, and re-layouts  4.68 us
    ppermute x1, starting transfers between devices, per_device(): got = lax.ppermute(send, 'seq_2', [(0, 1), (1, 0)])  4.11 us
    pallas_call x1, Pallas kernels, per_device(): pl.pallas_call(functools.partial(final_kernel, (width, chips, cores, core...  1.91 us
    pallas_call x1, Pallas kernels, per_device(): pl.pallas_call(functools.partial(squares_kernel, (width, chips, cores, ch...  1.86 us
  transfers between devices with their start and end apart: 1, of which 0 were waited for; matrix products, arithmetic and copies ran while one was open for 0% of the time, Pallas kernels for 0%

profile of v1, /device:TPU:1, one launch (start us, length us, event | category | flops | bytes accessed | tf_op | source)
XLA Modules:
  0.0 66.1 jit_solution(1510718427667671816)
XLA Ops:
  0.0 0.0 copy-start
  0.0 2.0 %copy.13.step_ref = bf16[2,10,8192]{2,1,0:T(8,128)(2,1)} copy(bf16[2,10,8192]{2,0,1:T(2,128)(2,1)} %param.6) | data formatting | bytes 655360 | tf_op args[0]
  2.0 0.0 copy-done
  2.0 0.0 copy-start.1
  2.0 1.0 %copy.14.inp_ref = bf16[2,10,8192]{2,1,0:T(8,128)(2,1)} copy(bf16[2,10,8192]{2,0,1:T(2,128)(2,1)S(1)} %copy-done) | data formatting | bytes 655360 | tf_op args[1]
  3.0 0.0 copy-done.1
  3.0 1.0 %copy.15.gate_ref = bf16[2,10,8192]{2,1,0:T(8,128)(2,1)} copy(bf16[2,10,8192]{2,0,1:T(2,128)(2,1)S(1)} %copy-done.1) | data formatting | bytes 655360 | tf_op args[2]
  4.0 12.0 %scan.1 = s32[704,128]{1,0:T(8,128)} custom-call(f32[640]{0:T(1024)} %rate_ref.1, s32[2,8]{1,0:T(2,128)} %reset_ref.1, bf16[2,10,8192]{2,1,0:T(8,128)(2,1)} %copy.13.step_ref, bf16[2,10,8192]{2,1,0:T(8,128)(2,1)} %copy.14.inp_ref, bf16[2,10,8192]{2,1,0:T(8,128)(2,1)} %copy.15.gate_ref), custom_call_target="tpu_custom_call" | custom-call | tf_op jit(solution)/shard_map/scan/pallas_call | solution.py:223
  16.0 27.2 %all_to_all.10 = s32[32,22,1,128]{3,2,1,0:T(1,128)} all-to-all(s32[32,22,1,128]{3,2,1,0:T(1,128)} %bitcast.3), channel_id=1, replica_groups=mesh['seq_0'=8,'seq_1'=4,'seq_2'=2,'chan'=8] {'seq_0','seq_1'}, dimensions={0} | all-to-all | bytes 720896 | tf_op jit(solution)/shard_map/all_to_all | solution.py:236
  43.2 1.9 %squares.1 = (f32[16,2,128]{2,1,0:T(2,128)}, s32[352,128]{1,0:T(8,128)}, s32[352,128]{1,0:T(8,128)}) custom-call(s32[704,128]{1,0:T(8,128)} %bitcast.4), custom_call_target="tpu_custom_call" | custom-call | tf_op jit(solution)/shard_map/squares/pallas_call | solution.py:239
  45.1 4.1 %collective-permute-start = (s32[352,128]{1,0:T(8,128)}, s32[352,128]{1,0:T(8,128)S(1)}, u32[]{:S(2)}, u32[]{:S(2)}) collective-permute-start(s32[352,128]{1,0:T(8,128)} %get-tuple-element.9), channel_id=1, source_target_pairs={{0,8},{8,0},{1,9},{9,1},{2,10},{10,2},{3,11},{11,3},{4,12},{12,4},... | collective-permute-start | bytes 540680 | tf_op jit(solution)/shard_map/ppermute | solution.py:247
  49.2 14.3 %all_to_all.11.sum_ref = f32[16,2,128]{2,1,0:T(2,128)} all-to-all(f32[16,2,128]{2,1,0:T(2,128)} %get-tuple-element.10), channel_id=1, replica_groups=mesh['seq_0'=8,'seq_1'=4,'seq_2'=2,'chan'=8] {'seq_2','chan'}, dimensions={0} | all-to-all | bytes 32768 | tf_op jit(solution)/shard_map/all_to_all | solution.py:246
  63.5 0.0 collective-permute-done.got_ref
  63.5 0.0 copy-start.2
  63.5 0.7 %copy-done.2 = s32[352,128]{1,0:T(8,128)} copy-done((s32[352,128]{1,0:T(8,128)}, s32[352,128]{1,0:T(8,128)S(1)}, u32[]{:S(2)}) %copy-start.2) | copy-done | bytes 180248
  64.2 1.9 %final.1 = bf16[2,640,128]{2,1,0:T(8,128)(2,1)} custom-call(s32[352,128]{1,0:T(8,128)} %get-tuple-element.8.keep_ref, s32[352,128]{1,0:T(8,128)} %copy-done.2, f32[16,2,128]{2,1,0:T(2,128)} %all_to_all.11.sum_ref, f32[5,128]{1,0:T(8,128)} %bitcast.5), custom_call_target="tpu_custom_call" | custom-call | tf_op jit(solution)/shard_map/final/pallas_call | solution.py:249
Async XLA Ops:
  0.0 2.0 %copy-start = (bf16[2,10,8192]{2,0,1:T(2,128)(2,1)S(1)}, bf16[2,10,8192]{2,0,1:T(2,128)(2,1)}, u32[]{:S(2)}) copy-start(bf16[2,10,8192]{2,0,1:T(2,128)(2,1)} %param.7) | copy-start | bytes 983044
  2.0 1.0 %copy-start.1 = (bf16[2,10,8192]{2,0,1:T(2,128)(2,1)S(1)}, bf16[2,10,8192]{2,0,1:T(2,128)(2,1)}, u32[]{:S(2)}) copy-start(bf16[2,10,8192]{2,0,1:T(2,128)(2,1)} %param.8) | copy-start | bytes 983044
  45.1 18.5 %collective-permute-start = (s32[352,128]{1,0:T(8,128)}, s32[352,128]{1,0:T(8,128)S(1)}, u32[]{:S(2)}, u32[]{:S(2)}) collective-permute-start(s32[352,128]{1,0:T(8,128)} %get-tuple-element.9), channel_id=1, source_target_pairs={{0,8},{8,0},{1,9},{9,1},{2,10},{10,2},{3,11},{11,3},{4,12},{12,4},... | collective-permute-start | bytes 540680 | tf_op jit(solution)/shard_map/ppermute | solution.py:247
  63.5 0.7 %copy-start.2 = (s32[352,128]{1,0:T(8,128)}, s32[352,128]{1,0:T(8,128)S(1)}, u32[]{:S(2)}) copy-start(s32[352,128]{1,0:T(8,128)S(1)} %collective-permute-done.got_ref) | copy-start | bytes 540676

commit v2 on v1

v2 whole, which is shorter than its diff:
```python
import functools
import math

import jax
import jax.numpy as jnp
from jax import lax
from jax.experimental import pallas as pl
from jax.experimental.pallas import tpu as pltpu
from jax.sharding import Mesh
from jax.sharding import PartitionSpec as P

FEATURE_WIDTH = 5120
SEQ = ("seq_0", "seq_1", "seq_2")
CHAN_SEQ = ("chan", "seq_0", "seq_1", "seq_2")
LANES = 128
SUB = 8
LEVELS = 32700.0
MIDDLE = 32768.0
FINE = 64.0
CODE_ZERO = 16384.0
LOG2E = 1.4426950408889634
UNROLL = 2


def root_of_one_minus_exp(x, expo):
    p = 1.0 / 6.0 - x * (1.0 / 24.0 - x * (1.0 / 120.0))
    p = x * (1.0 - x * (0.5 - x * p))
    y = jnp.where(x < 0.0625, p, 1.0 - expo * expo)
    return y * lax.rsqrt(jnp.maximum(y, 1e-37))


def tile(v):
    return slice(v * SUB, (v + 1) * SUB)


def scan_kernel(
    sizes, rate_ref, reset_ref, step_ref, inp_ref, gate_ref, out_ref, part, held, live, top, tot, ints
):
    batch, width, blocks, ndoc = sizes
    place = lax.axis_index(SEQ)
    count = batch * blocks
    tiles = LANES // SUB
    lane = lax.broadcasted_iota(jnp.int32, (SUB, LANES), 1)
    sub = lax.broadcasted_iota(jnp.int32, (SUB, LANES), 0)
    odd = (sub & 1) == 1

    marks = [jnp.where(odd, reset_ref[1, k], reset_ref[0, k]) for k in range(ndoc)]
    for v in range(tiles):
        t = (v * (SUB // 2) + (sub >> 1)) * LANES + lane
        hit = t == marks[0]
        for mark in marks[1:]:
            hit = hit | (t == mark)
        live[tile(v), :] = jnp.where(hit, 0.0, 1.0)
        top[tile(v), :] = jnp.full((SUB, LANES), 1e-37, jnp.float32)
        part[tile(v), :] = jnp.zeros((SUB, LANES), jnp.float32)
    tot[...] = jnp.zeros_like(tot)

    def local(c, _):
        at = pl.ds(pl.multiple_of(c * count, count), count)
        scaled = step_ref[at, :].astype(jnp.float32) * rate_ref[place * width + c]
        expo = jnp.exp2(scaled * (-LOG2E))
        drive = root_of_one_minus_exp(scaled + scaled, expo) * inp_ref[at, :].astype(jnp.float32)
        at_a = (expo * live[...]).T
        at_s = drive.T
        end_a = end_s = None
        for v in range(tiles):
            a, s = at_a[tile(v)], at_s[tile(v)]
            for k in (1, 2, 4):
                keep = sub >= k
                s = s + a * jnp.where(keep, pltpu.roll(s, k, 0), 0.0)
                a = a * jnp.where(keep, pltpu.roll(a, k, 0), 1.0)
            if v:
                s = s + a * end_s
                a = a * end_a
            here = pl.ds(pl.multiple_of(c * count + v * SUB, SUB), SUB)
            held[0, here, :] = a
            held[1, here, :] = s
            end_a = jnp.broadcast_to(a[SUB - 1 :], (SUB, LANES))
            end_s = jnp.broadcast_to(s[SUB - 1 :], (SUB, LANES))
        tot[0, pl.ds(c, 1), :] = end_a[:1]
        tot[1, pl.ds(c, 1), :] = end_s[:1]
        return 0

    lax.fori_loop(0, width, local, 0, unroll=UNROLL)

    wide = lax.broadcasted_iota(jnp.int32, tot.shape[1:], 1)
    a, s = tot[0], tot[1]
    k = batch
    while k < count:
        keep = wide >= k
        s = s + a * jnp.where(keep, pltpu.roll(s, k, 1), 0.0)
        a = a * jnp.where(keep, pltpu.roll(a, k, 1), 1.0)
        k *= 2
    tot[0] = jnp.where(wide >= batch, pltpu.roll(s, batch, 1), 0.0)

    def emit(c, _):
        at = pl.ds(pl.multiple_of(c * count, count), count)
        state = (held[1, at, :] + held[0, at, :] * tot[0, pl.ds(c, 1), :]).T
        g = gate_ref[at, :].astype(jnp.float32)
        value = state * (g / (1.0 + jnp.exp2(g * (-LOG2E))))
        held[2, at, :] = value
        top[...] = jnp.maximum(top[...], jnp.abs(value))
        part[...] = part[...] + value * value
        return 0

    lax.fori_loop(0, width, emit, 0, unroll=UNROLL)

    e = jnp.ceil(jnp.log2(top[...]) * FINE)
    top[...] = jnp.exp2(e * (-1.0 / FINE)) * LEVELS
    ints[pl.ds(width * count, count), :] = (e + CODE_ZERO).astype(jnp.int32)
    for c in range(width):
        ints[tile_of(c, count), :] = (held[2, tile_of(c, count), :] * top[...] + (MIDDLE + 0.5)).astype(
            jnp.int32
        )
    for c in range(width + 1):
        for m in range(blocks // SUB):
            first = ints[pl.ds(c * count + m * SUB * batch, SUB, stride=batch), :]
            second = ints[pl.ds(c * count + m * SUB * batch + 1, SUB, stride=batch), :]
            out_ref[pl.ds(m * SUB * (width + 1) + c, SUB, stride=width + 1), :] = (
                first * 65536 | second
            )


def tile_of(c, count):
    return slice(c * count, (c + 1) * count)


def opened(word):
    return (
        lax.shift_right_logical(word, 16).astype(jnp.float32),
        (word & 65535).astype(jnp.float32),
    )


def scales(word):
    return [jnp.exp2((e - CODE_ZERO) * (1.0 / FINE)) * (1.0 / LEVELS) for e in opened(word)]


def squares_kernel(sizes, got_ref, sum_ref, keep_ref, send_ref):
    width, chips, cores, chan = sizes
    mine = lax.axis_index("seq_2")
    record = width + 1
    acc = [[None, None], [None, None]]
    for m in range(chips // SUB):
        base = m * SUB * cores * record
        codes = [
            got_ref[pl.ds(base + k * record + width, SUB, stride=cores * record), :]
            for k in range(cores)
        ]
        scale = [scales(w) for w in codes]
        for c in range(record):
            words = [
                got_ref[pl.ds(base + k * record + c, SUB, stride=cores * record), :]
                for k in range(cores)
            ]
            to = pl.ds(m * SUB * record + c, SUB, stride=record)
            keep_ref[to, :] = jnp.where(mine == 0, words[0], words[1])
            send_ref[to, :] = jnp.where(mine == 0, words[1], words[0])
            if c < width:
                for k in range(cores):
                    for b, q in enumerate(opened(words[k])):
                        v = (q - MIDDLE) * scale[k][b]
                        acc[k][b] = v * v if acc[k][b] is None else acc[k][b] + v * v
    for k in range(cores):
        for b in range(2):
            row = jnp.sum(acc[k][b], axis=0, keepdims=True)
            for y in range(chan):
                sum_ref[k * chan + y, b : b + 1, :] = row


def final_kernel(sizes, keep_ref, got_ref, sum_ref, gain_ref, out_ref, flat):
    width, chips, cores, peers = sizes
    mine = lax.axis_index("seq_2")
    record = width + 1
    total = sum_ref[0]
    for k in range(1, peers):
        total = total + sum_ref[k]
    norm = lax.rsqrt(total / jnp.float32(FEATURE_WIDTH) + 1e-5)
    for m in range(chips // SUB):
        def words(c):
            at = pl.ds(m * SUB * record + c, SUB, stride=record)
            a, b = keep_ref[at, :], got_ref[at, :]
            return jnp.where(mine == 0, a, b), jnp.where(mine == 0, b, a)

        scale = [scales(w) for w in words(width)]
        scale = [[s * norm[b : b + 1] for b, s in enumerate(pair)] for pair in scale]
        for c in range(width):
            for k, word in enumerate(words(c)):
                for b, q in enumerate(opened(word)):
                    row = m * SUB * cores * width + k * width + c
                    flat[b, pl.ds(row, SUB, stride=cores * width), :] = (q - MIDDLE) * scale[k][b]
    channels = out_ref.shape[1]
    for g in range(channels // LANES):
        gain = jnp.broadcast_to(gain_ref[g : g + 1, :], (LANES, LANES)).T
        for b in range(2):
            rows = slice(g * LANES, (g + 1) * LANES)
            out_ref[b, rows, :] = (flat[b, rows, :] * gain).astype(jnp.bfloat16)


def whole(space=pltpu.VMEM):
    return pl.BlockSpec(memory_space=space)


def room(mebibytes):
    return pltpu.CompilerParams(vmem_limit_bytes=mebibytes * 1024 * 1024)


def per_device(step_size, inputs, gate_input, decay_rate, norm_gain, resets):
    batch, width, length = step_size.shape
    chips = lax.axis_size("seq_0") * lax.axis_size("seq_1")
    cores = lax.axis_size("seq_2")
    chan = lax.axis_size("chan")
    blocks = chips * cores
    record = width + 1
    rows = batch * width * blocks

    def as_rows(array):
        split = array.reshape(batch, width, blocks, LANES)
        return split.transpose(1, 2, 0, 3).reshape(rows, LANES)

    words, part = pl.pallas_call(
        functools.partial(scan_kernel, (batch, width, blocks, resets.shape[1])),
        out_shape=(
            jax.ShapeDtypeStruct((blocks * record, LANES), jnp.int32),
            jax.ShapeDtypeStruct((batch * blocks, LANES), jnp.float32),
        ),
        in_specs=[whole(pltpu.SMEM), whole(pltpu.SMEM), whole(), whole(), whole()],
        out_specs=(whole(), whole()),
        scratch_shapes=[
            pltpu.VMEM((3, rows, LANES), jnp.float32),
            pltpu.VMEM((batch * blocks, LANES), jnp.float32),
            pltpu.VMEM((batch * blocks, LANES), jnp.float32),
            pltpu.VMEM((2, 2 * SUB, LANES), jnp.float32),
            pltpu.VMEM((rows + batch * blocks, LANES), jnp.int32),
        ],
        compiler_params=room(16),
        name="scan",
    )(decay_rate, resets, as_rows(step_size), as_rows(inputs), as_rows(gate_input))
    words = words.reshape(chips, cores * record, 1, LANES)
    words = lax.all_to_all(words, ("seq_0", "seq_1"), 0, 0, tiled=True)
    words = words.reshape(chips * cores * record, LANES)
    half = jax.ShapeDtypeStruct((chips * record, LANES), jnp.int32)
    sums, keep, send = pl.pallas_call(
        functools.partial(squares_kernel, (width, chips, cores, chan)),
        out_shape=(jax.ShapeDtypeStruct((cores * chan, batch, LANES), jnp.float32), half, half),
        in_specs=[whole()],
        out_specs=(whole(), whole(), whole()),
        compiler_params=room(8),
        name="squares",
    )(words)
    sums = lax.all_to_all(sums, ("seq_2", "chan"), 0, 0, tiled=True)
    got = lax.ppermute(send, "seq_2", [(0, 1), (1, 0)])
    channels = chips * cores * width
    return pl.pallas_call(
        functools.partial(final_kernel, (width, chips, cores, cores * chan)),
        out_shape=jax.ShapeDtypeStruct((batch, channels, LANES), jnp.bfloat16),
        in_specs=[whole()] * 4,
        out_specs=whole(),
        scratch_shapes=[pltpu.VMEM((batch, channels, LANES), jnp.float32)],
        compiler_params=room(8),
        name="final",
    )(keep, got, sums, norm_gain.reshape(channels // LANES, LANES))


def solution(mesh):
    split = Mesh(
        mesh.devices.reshape(8, 4, 2, mesh.shape["chan"]), ("seq_0", "seq_1", "seq_2", "chan")
    )
    in_specs = (
        P(None, CHAN_SEQ, None),
        P(None, CHAN_SEQ, None),
        P(None, CHAN_SEQ, None),
        P("chan"),
        P("chan"),
        P(),
    )
    out_specs = P(None, "chan", SEQ)
    return jax.shard_map(
        per_device, mesh=split, in_specs=in_specs, out_specs=out_specs, check_vma=False
    )
```

time: 66.5 us -> 53.8 us (0.81)
  Pallas kernels: 15.8 us -> 4.82 us
  local copies, waits for them, and re-layouts: 4.68 us -> 3.62 us
    pallas_call x1, Pallas kernels: 12 us -> 3.76 us  [per_device(): pl.pallas_call(functools.partial(scan_kernel, (batch, width, blocks, rese...]
    pallas_call x1, Pallas kernels: 1.86 us -> 0.17 us  [per_device(): pl.pallas_call(functools.partial(squares_kernel, (width, chips, cores, ch...]
    unnamed x9 -> x12, local copies, waits for them, and re-layouts: 4.68 us -> 3.62 us
    pallas_call x1, Pallas kernels: 1.91 us -> 0.9 us  [per_device(): pl.pallas_call(functools.partial(final_kernel, (width, chips, cores, core...]
where the time goes in v2:
time: 53.8 us; the launch traced here: 53.5 us
  blocking collectives  40.9 us (76%)
  Pallas kernels  4.82 us (9%)
  starting transfers between devices  4.12 us (8%)
  local copies, waits for them, and re-layouts  3.62 us (7%)
    all_to_all x1, blocking collectives, per_device(): words = lax.all_to_all(words, ('seq_0', 'seq_1'), 0, 0, tiled=True)  26.9 us
    all_to_all x1, blocking collectives, per_device(): sums = lax.all_to_all(sums, ('seq_2', 'chan'), 0, 0, tiled=True)  14 us
    ppermute x1, starting transfers between devices, per_device(): got = lax.ppermute(send, 'seq_2', [(0, 1), (1, 0)])  4.12 us
    pallas_call x1, Pallas kernels, per_device(): pl.pallas_call(functools.partial(scan_kernel, (batch, width, blocks, rese...  3.76 us
    unnamed x12, local copies, waits for them, and re-layouts  3.62 us
  transfers between devices with their start and end apart: 1, of which 0 were waited for; matrix products, arithmetic and copies ran while one was open for 0% of the time, Pallas kernels for 0%

profile of v2, /device:TPU:1, one launch (start us, length us, event | category | flops | bytes accessed | tf_op | source)
XLA Modules:
  0.0 53.5 jit_solution(5380528103724975361)
XLA Ops:
  0.0 0.0 copy-start.3
  0.0 0.0 copy-start.5
  0.0 0.7 %copy-done.3 = f32[640]{0:T(1024)S(1)} copy-done((f32[640]{0:T(1024)S(1)}, f32[640]{0:T(1024)}, u32[]{:S(2)}) %copy-start.3) | copy-done | bytes 2584
  0.7 0.0 copy-done.5
  0.7 0.0 copy-start
  0.7 1.0 %copy-done = bf16[2,10,8192]{2,0,1:T(2,128)(2,1)S(1)} copy-done((bf16[2,10,8192]{2,0,1:T(2,128)(2,1)S(1)}, bf16[2,10,8192]{2,0,1:T(2,128)(2,1)}, u32[]{:S(2)}) %copy-start) | copy-done | bytes 327704
  1.7 0.0 copy-start.1
  1.7 1.0 %copy-done.1 = bf16[2,10,8192]{2,0,1:T(2,128)(2,1)S(1)} copy-done((bf16[2,10,8192]{2,0,1:T(2,128)(2,1)S(1)}, bf16[2,10,8192]{2,0,1:T(2,128)(2,1)}, u32[]{:S(2)}) %copy-start.1) | copy-done | bytes 327704
  2.6 0.0 copy-start.2
  2.6 1.0 %copy-done.2 = bf16[2,10,8192]{2,0,1:T(2,128)(2,1)S(1)} copy-done((bf16[2,10,8192]{2,0,1:T(2,128)(2,1)S(1)}, bf16[2,10,8192]{2,0,1:T(2,128)(2,1)}, u32[]{:S(2)}) %copy-start.2) | copy-done | bytes 327704
  3.6 3.8 %scan.1 = (s32[704,128]{1,0:T(8,128)S(1)}, f32[128,128]{1,0:T(8,128)}) custom-call(f32[640]{0:T(1024)S(1)} %copy-done.3, s32[2,8]{1,0:T(2,128)S(1)} %copy-done.5, bf16[1280,128]{1,0:T(8,128)(2,1)S(1)} %bitcast.20, bf16[1280,128]{1,0:T(8,128)(2,1)S(1)} %bitcast.21, bf16[1280,128]{1,0:T(8,128)(2,1)S(1)} %bitcast.22), custom_call_target="tpu_custom_call" | custom-call | tf_op jit(solution)/shard_map/scan/pallas_call | solution.py:221
  7.4 26.9 %all_to_all.10 = s32[32,22,1,128]{3,2,1,0:T(1,128)S(1)} all-to-all(s32[32,22,1,128]{3,2,1,0:T(1,128)S(1)} %bitcast.19), channel_id=1, replica_groups=mesh['seq_0'=8,'seq_1'=4,'seq_2'=2,'chan'=8] {'seq_0','seq_1'}, dimensions={0} | all-to-all | bytes 720896 | tf_op jit(solution)/shard_map/all_to_all | solution.py:240
  34.2 0.2 squares.1
  34.4 4.1 %collective-permute-start = (s32[352,128]{1,0:T(8,128)S(1)}, s32[352,128]{1,0:T(8,128)S(1)}, u32[]{:S(2)}, u32[]{:S(2)}) collective-permute-start(s32[352,128]{1,0:T(8,128)S(1)} %get-tuple-element.11), channel_id=1, source_target_pairs={{0,8},{8,0},{1,9},{9,1},{2,10},{10,2},{3,11},{11,3},{4,12},{12,4},... | collective-permute-start | bytes 540680 | tf_op jit(solution)/shard_map/ppermute | solution.py:252
  38.5 0.0 copy-start.4
  38.5 14.0 %all_to_all.11.sum_ref = f32[16,2,128]{2,1,0:T(2,128)S(1)} all-to-all(f32[16,2,128]{2,1,0:T(2,128)S(1)} %get-tuple-element.12), channel_id=1, replica_groups=mesh['seq_0'=8,'seq_1'=4,'seq_2'=2,'chan'=8] {'seq_2','chan'}, dimensions={0} | all-to-all | bytes 32768 | tf_op jit(solution)/shard_map/all_to_all | solution.py:251
  52.6 0.0 collective-permute-done.got_ref
  52.6 0.0 copy-done.4
  52.6 0.9 %final.1 = bf16[2,640,128]{2,1,0:T(8,128)(2,1)} custom-call(s32[352,128]{1,0:T(8,128)S(1)} %get-tuple-element.10.keep_ref, s32[352,128]{1,0:T(8,128)S(1)} %collective-permute-done.got_ref, f32[16,2,128]{2,1,0:T(2,128)S(1)} %all_to_all.11.sum_ref, f32[5,128]{1,0:T(8,128)S(1)} %bitcast.23), custom_call_target="tpu_custom_call" | custom-call | tf_op jit(solution)/shard_map/final/pallas_call | solution.py:254
Async XLA Ops:
  0.0 0.7 %copy-start.3 = (f32[640]{0:T(1024)S(1)}, f32[640]{0:T(1024)}, u32[]{:S(2)}) copy-start(f32[640]{0:T(1024)} %rate_ref.1) | copy-start | bytes 7684
  0.0 0.7 %copy-start.5 = (s32[2,8]{1,0:T(2,128)S(1)}, s32[2,8]{1,0:T(2,128)}, u32[]{:S(2)}) copy-start(s32[2,8]{1,0:T(2,128)} %reset_ref.1) | copy-start | bytes 196
  0.7 1.0 %copy-start = (bf16[2,10,8192]{2,0,1:T(2,128)(2,1)S(1)}, bf16[2,10,8192]{2,0,1:T(2,128)(2,1)}, u32[]{:S(2)}) copy-start(bf16[2,10,8192]{2,0,1:T(2,128)(2,1)} %param.6) | copy-start | bytes 983044
  1.7 1.0 %copy-start.1 = (bf16[2,10,8192]{2,0,1:T(2,128)(2,1)S(1)}, bf16[2,10,8192]{2,0,1:T(2,128)(2,1)}, u32[]{:S(2)}) copy-start(bf16[2,10,8192]{2,0,1:T(2,128)(2,1)} %param.7) | copy-start | bytes 983044
  2.6 1.0 %copy-start.2 = (bf16[2,10,8192]{2,0,1:T(2,128)(2,1)S(1)}, bf16[2,10,8192]{2,0,1:T(2,128)(2,1)}, u32[]{:S(2)}) copy-start(bf16[2,10,8192]{2,0,1:T(2,128)(2,1)} %param.8) | copy-start | bytes 983044
  34.4 18.2 %collective-permute-start = (s32[352,128]{1,0:T(8,128)S(1)}, s32[352,128]{1,0:T(8,128)S(1)}, u32[]{:S(2)}, u32[]{:S(2)}) collective-permute-start(s32[352,128]{1,0:T(8,128)S(1)} %get-tuple-element.11), channel_id=1, source_target_pairs={{0,8},{8,0},{1,9},{9,1},{2,10},{10,2},{3,11},{11,3},{4,12},{12,4},... | collective-permute-start | bytes 540680 | tf_op jit(solution)/shard_map/ppermute | solution.py:252
  38.5 14.1 %copy-start.4 = (f32[640]{0:T(1024)S(1)}, f32[640]{0:T(1024)}, u32[]{:S(2)}) copy-start(f32[640]{0:T(1024)} %param.10) | copy-start | bytes 7684

commit v3 on v2

v3 whole, which is shorter than its diff:
```python
import functools

import jax
import jax.numpy as jnp
from jax import lax
from jax.experimental import pallas as pl
from jax.experimental.pallas import tpu as pltpu
from jax.sharding import Mesh
from jax.sharding import PartitionSpec as P


FEATURE_WIDTH = 5120
SEQ = ("seq_0", "seq_1", "seq_2")
CHAN_SEQ = ("chan", "seq_0", "seq_1", "seq_2")
LANES = 128
SUB = 8
LEVELS = 32700.0
MIDDLE = 32768.0
FINE = 64.0
CODE_ZERO = 16384.0
CORES = 2
LOG2E = 1.4426950408889634
UNROLL = 2


def root_of_one_minus_exp(x, expo):
    p = 1.0 / 6.0 - x * (1.0 / 24.0 - x * (1.0 / 120.0))
    p = x * (1.0 - x * (0.5 - x * p))
    y = jnp.where(x < 0.0625, p, 1.0 - expo * expo)
    return y * lax.rsqrt(jnp.maximum(y, 1e-37))


def tile(v):
    return slice(v * SUB, (v + 1) * SUB)


def scan_kernel(
    sizes,
    rate_hbm,
    reset_hbm,
    step_hbm,
    inp_hbm,
    gate_hbm,
    out_ref,
    held,
    live,
    top,
    tot,
    ints,
    step_ref,
    inp_ref,
    gate_ref,
    rate_ref,
    reset_ref,
    sems,
    small,
):
    batch, width, blocks, ndoc = sizes
    place = lax.axis_index(SEQ)
    count = batch * blocks
    tiles = LANES // SUB
    lane = lax.broadcasted_iota(jnp.int32, (SUB, LANES), 1)
    sub = lax.broadcasted_iota(jnp.int32, (SUB, LANES), 0)
    odd = (sub & 1) == 1

    sources = ((step_hbm, step_ref), (inp_hbm, inp_ref), (gate_hbm, gate_ref))

    def fetch(k, c):
        at = pl.ds(pl.multiple_of(c * count, count), count)
        return pltpu.make_async_copy(sources[k][0].at[at], sources[k][1].at[at], sems.at[k, c])

    scalars = [
        pltpu.make_async_copy(rate_hbm, rate_ref, small.at[0]),
        pltpu.make_async_copy(reset_hbm, reset_ref, small.at[1]),
    ]
    for copy in scalars:
        copy.start()
    for c in range(width):
        fetch(0, c).start()
        fetch(1, c).start()
    for c in range(width):
        fetch(2, c).start()

    for copy in scalars:
        copy.wait()
    marks = [jnp.where(odd, reset_ref[1, k], reset_ref[0, k]) for k in range(ndoc)]
    for v in range(tiles):
        t = (v * (SUB // 2) + (sub >> 1)) * LANES + lane
        hit = t == marks[0]
        for mark in marks[1:]:
            hit = hit | (t == mark)
        live[tile(v), :] = jnp.where(hit, 0.0, 1.0)
        top[tile(v), :] = jnp.full((SUB, LANES), 1e-37, jnp.float32)
    tot[...] = jnp.zeros_like(tot)

    def local(c, _):
        at = pl.ds(pl.multiple_of(c * count, count), count)
        fetch(0, c).wait()
        fetch(1, c).wait()
        scaled = step_ref[at, :].astype(jnp.float32) * rate_ref[place * width + c]
        expo = jnp.exp2(scaled * (-LOG2E))
        drive = root_of_one_minus_exp(scaled + scaled, expo) * inp_ref[at, :].astype(jnp.float32)
        at_a = (expo * live[...]).T
        at_s = drive.T
        end_a = end_s = None
        for v in range(tiles):
            a, s = at_a[tile(v)], at_s[tile(v)]
            for k in (1, 2, 4):
                keep = sub >= k
                s = s + a * jnp.where(keep, pltpu.roll(s, k, 0), 0.0)
                a = a * jnp.where(keep, pltpu.roll(a, k, 0), 1.0)
            if v:
                s = s + a * end_s
                a = a * end_a
            here = pl.ds(pl.multiple_of(c * count + v * SUB, SUB), SUB)
            held[0, here, :] = a
            held[1, here, :] = s
            end_a = jnp.broadcast_to(a[SUB - 1 :], (SUB, LANES))
            end_s = jnp.broadcast_to(s[SUB - 1 :], (SUB, LANES))
        tot[0, pl.ds(c, 1), :] = end_a[:1]
        tot[1, pl.ds(c, 1), :] = end_s[:1]
        return 0

    lax.fori_loop(0, width, local, 0, unroll=UNROLL)

    wide = lax.broadcasted_iota(jnp.int32, tot.shape[1:], 1)
    a, s = tot[0], tot[1]
    k = batch
    while k < count:
        keep = wide >= k
        s = s + a * jnp.where(keep, pltpu.roll(s, k, 1), 0.0)
        a = a * jnp.where(keep, pltpu.roll(a, k, 1), 1.0)
        k *= 2
    tot[0] = jnp.where(wide >= batch, pltpu.roll(s, batch, 1), 0.0)

    def emit(c, _):
        at = pl.ds(pl.multiple_of(c * count, count), count)
        state = (held[1, at, :] + held[0, at, :] * tot[0, pl.ds(c, 1), :]).T
        fetch(2, c).wait()
        g = gate_ref[at, :].astype(jnp.float32)
        value = state * (g / (1.0 + jnp.exp2(g * (-LOG2E))))
        held[2, at, :] = value
        top[...] = jnp.maximum(top[...], jnp.abs(value))
        return 0

    lax.fori_loop(0, width, emit, 0, unroll=UNROLL)

    e = jnp.ceil(jnp.log2(top[...]) * FINE)
    top[...] = jnp.exp2(e * (-1.0 / FINE)) * LEVELS
    ints[pl.ds(width * count, count), :] = (e + CODE_ZERO).astype(jnp.int32)
    for c in range(width):
        ints[tile_of(c, count), :] = (held[2, tile_of(c, count), :] * top[...] + (MIDDLE + 0.5)).astype(
            jnp.int32
        )
    record = width + 1
    for c in range(record):
        for m in range(blocks // SUB):
            base = c * count + m * SUB * batch
            first, second = [ints[pl.ds(base + b, SUB, stride=batch), :] for b in range(batch)]
            out_ref[pl.ds(m * SUB * record + c, SUB, stride=record), :] = first * 65536 | second


def tile_of(c, count):
    return slice(c * count, (c + 1) * count)


def opened(word):
    return (
        lax.shift_right_logical(word, 16).astype(jnp.float32),
        (word & 65535).astype(jnp.float32),
    )


def scales(word):
    return [jnp.exp2((e - CODE_ZERO) * (1.0 / FINE)) * (1.0 / LEVELS) for e in opened(word)]


def words_at(ref, m, k, c, record):
    return ref[pl.ds((m * SUB * CORES + k) * record + c, SUB, stride=CORES * record), :]


def squares_kernel(sizes, got_ref, sum_ref):
    width, chips = sizes
    record = width + 1
    chan = sum_ref.shape[0] // CORES
    for k in range(CORES):
        acc = [None, None]
        for m in range(chips // SUB):
            scale = scales(words_at(got_ref, m, k, width, record))
            part = [None, None]
            for c in range(width):
                for b, q in enumerate(opened(words_at(got_ref, m, k, c, record))):
                    v = q - MIDDLE
                    part[b] = v * v if part[b] is None else part[b] + v * v
            for b in range(2):
                more = part[b] * (scale[b] * scale[b])
                acc[b] = more if acc[b] is None else acc[b] + more
        for b in range(2):
            row = jnp.sum(acc[b], axis=0, keepdims=True)
            for y in range(chan):
                sum_ref[k * chan + y, b : b + 1, :] = row


def gain_kernel(gain_ref, out_ref):
    for g in range(out_ref.shape[0] // LANES):
        row = gain_ref[g : g + 1, :]
        out_ref[g * LANES : (g + 1) * LANES, :] = jnp.broadcast_to(row, (LANES, LANES)).T


def final_kernel(sizes, own_ref, mate_ref, sum_ref, gain_ref, out_ref, flat):
    width, chips = sizes
    mine = lax.axis_index("seq_2")
    record = width + 1
    total = sum_ref[0]
    for k in range(1, sum_ref.shape[0]):
        total = total + sum_ref[k]
    norm = lax.rsqrt(total / jnp.float32(FEATURE_WIDTH) + 1e-5)
    for m in range(chips // SUB):

        def words(c):
            a = words_at(own_ref, m, mine, c, record)
            b = words_at(mate_ref, m, mine, c, record)
            return jnp.where(mine == 0, a, b), jnp.where(mine == 0, b, a)

        scale = [scales(w) for w in words(width)]
        scale = [[s * norm[b : b + 1] for b, s in enumerate(pair)] for pair in scale]
        for c in range(width):
            for k, word in enumerate(words(c)):
                for b, q in enumerate(opened(word)):
                    row = (m * SUB * CORES + k) * width + c
                    flat[b, pl.ds(row, SUB, stride=CORES * width), :] = (q - MIDDLE) * scale[k][b]
    for b in range(2):
        out_ref[b] = (flat[b] * gain_ref[...]).astype(jnp.bfloat16)


def whole(space=pltpu.VMEM):
    return pl.BlockSpec(memory_space=space)


def room(mebibytes):
    return pltpu.CompilerParams(vmem_limit_bytes=mebibytes * 1024 * 1024)


def per_device(step_size, inputs, gate_input, decay_rate, norm_gain, resets):
    batch, width, _ = step_size.shape
    chips = lax.axis_size("seq_0") * lax.axis_size("seq_1")
    cores = lax.axis_size("seq_2")
    chan = lax.axis_size("chan")
    blocks = chips * cores
    record = width + 1
    rows = batch * width * blocks

    def as_rows(array):
        split = array.reshape(batch, width, blocks, LANES)
        return split.transpose(1, 2, 0, 3).reshape(rows, LANES)

    words = pl.pallas_call(
        functools.partial(scan_kernel, (batch, width, blocks, resets.shape[1])),
        out_shape=jax.ShapeDtypeStruct((blocks * record, LANES), jnp.int32),
        in_specs=[whole(pltpu.HBM)] * 5,
        out_specs=whole(),
        scratch_shapes=[
            pltpu.VMEM((3, rows, LANES), jnp.float32),
            pltpu.VMEM((batch * blocks, LANES), jnp.float32),
            pltpu.VMEM((batch * blocks, LANES), jnp.float32),
            pltpu.VMEM((2, 2 * SUB, LANES), jnp.float32),
            pltpu.VMEM((rows + batch * blocks, LANES), jnp.int32),
            *[pltpu.VMEM((rows, LANES), jnp.bfloat16)] * 3,
            pltpu.SMEM(decay_rate.shape, jnp.float32),
            pltpu.SMEM(resets.shape, jnp.int32),
            pltpu.SemaphoreType.DMA((3, width)),
            pltpu.SemaphoreType.DMA((2,)),
        ],
        compiler_params=room(16),
        name="scan",
    )(
        *[
            pltpu.with_memory_space_constraint(x, pltpu.HBM)
            for x in (decay_rate, resets, *map(as_rows, (step_size, inputs, gate_input)))
        ],
    )
    words = words.reshape(chips, cores * record, 1, LANES)
    words = lax.all_to_all(words, ("seq_0", "seq_1"), 0, 0, tiled=True)
    words = words.reshape(blocks * record, LANES)
    sums = pl.pallas_call(
        functools.partial(squares_kernel, (width, chips)),
        out_shape=jax.ShapeDtypeStruct((cores * chan, batch, LANES), jnp.float32),
        in_specs=[whole()],
        out_specs=whole(),
        compiler_params=room(8),
        name="squares",
    )(words)
    sums = lax.all_to_all(sums, ("seq_2", "chan"), 0, 0, tiled=True)
    mate = lax.ppermute(words, "seq_2", [(0, 1), (1, 0)])
    channels = blocks * width
    gain = pl.pallas_call(
        gain_kernel,
        out_shape=jax.ShapeDtypeStruct((channels, LANES), jnp.float32),
        in_specs=[whole()],
        out_specs=whole(),
        compiler_params=room(8),
        name="gain",
    )(norm_gain.reshape(channels // LANES, LANES))
    return pl.pallas_call(
        functools.partial(final_kernel, (width, chips)),
        out_shape=jax.ShapeDtypeStruct((batch, channels, LANES), jnp.bfloat16),
        in_specs=[whole()] * 4,
        out_specs=whole(),
        scratch_shapes=[pltpu.VMEM((batch, channels, LANES), jnp.float32)],
        compiler_params=room(8),
        name="final",
    )(words, mate, sums, gain)


def solution(mesh):
    split = Mesh(
        mesh.devices.reshape(8, 4, 2, mesh.shape["chan"]), ("seq_0", "seq_1", "seq_2", "chan")
    )
    in_specs = (
        P(None, CHAN_SEQ, None),
        P(None, CHAN_SEQ, None),
        P(None, CHAN_SEQ, None),
        P("chan"),
        P("chan"),
        P(),
    )
    out_specs = P(None, "chan", SEQ)

    return jax.shard_map(
        per_device, mesh=split, in_specs=in_specs, out_specs=out_specs, check_vma=False
    )
```

time: 53.8 us -> 52.1 us (0.968)
  blocking collectives: 40.9 us -> 26.9 us
  starting transfers between devices: 4.12 us -> 11.5 us
  waiting for transfers between devices: 0.01 us -> 6.85 us
  local copies, waits for them, and re-layouts: 3.62 us -> 0.01 us
  Pallas kernels: 4.82 us -> 6.58 us
    all_to_all x1 -> x0, blocking collectives: 14 us -> none  [per_device(): sums = lax.all_to_all(sums, ('seq_2', 'chan'), 0, 0, tiled=True)]
    all_to_all x0 -> x1, starting transfers between devices: none -> 7.36 us  [per_device(): sums = lax.all_to_all(sums, ('seq_2', 'chan'), 0, 0, tiled=True)]
    all_to_all x0 -> x1, waiting for transfers between devices: none -> 6.84 us  [per_device(): sums = lax.all_to_all(sums, ('seq_2', 'chan'), 0, 0, tiled=True)]
    unnamed x12 -> x2, local copies, waits for them, and re-layouts: 3.62 us -> 0.01 us
    pallas_call x1, Pallas kernels: 3.76 us -> 4.75 us  [per_device(): pl.pallas_call(functools.partial(scan_kernel, (batch, width, blocks, rese...]
    pallas_call x2 -> x3, Pallas kernels: 1.07 us -> 1.83 us  [the longest x1 0.93 us: per_device(): pl.pallas_call(functools.partial(final_kernel, (width, chips)), out_shape...]
  transfers between devices with their start and end apart: 1 -> 2, of which waited for: 0 -> 1; matrix products, arithmetic and copies ran while one was open for 0% -> 0% of each run, Pallas kernels for 0% -> 2%
where the time goes in v3:
time: 52.1 us; the launch traced here: 51.8 us
  blocking collectives  26.9 us (52%)
  starting transfers between devices  11.5 us (22%)
  waiting for transfers between devices  6.85 us (13%)
  Pallas kernels  6.58 us (13%)
    all_to_all x1, blocking collectives, per_device(): words = lax.all_to_all(words, ('seq_0', 'seq_1'), 0, 0, tiled=True)  26.9 us
    all_to_all x1, starting transfers between devices, per_device(): sums = lax.all_to_all(sums, ('seq_2', 'chan'), 0, 0, tiled=True)  7.36 us
    all_to_all x1, waiting for transfers between devices, per_device(): sums = lax.all_to_all(sums, ('seq_2', 'chan'), 0, 0, tiled=True)  6.84 us
    pallas_call x1, Pallas kernels, per_device(): pl.pallas_call(functools.partial(scan_kernel, (batch, width, blocks, rese...  4.75 us
    ppermute x1, starting transfers between devices, per_device(): mate = lax.ppermute(words, 'seq_2', [(0, 1), (1, 0)])  4.11 us
  transfers between devices with their start and end apart: 2, of which 1 were waited for; matrix products, arithmetic and copies ran while one was open for 0% of the time, Pallas kernels for 2%

profile of v3, /device:TPU:1, one launch (start us, length us, event | category | flops | bytes accessed | tf_op | source)
XLA Modules:
  0.0 51.8 jit_solution(16463174758796578900)
XLA Ops:
  0.0 4.7 %scan.1 = s32[704,128]{1,0:T(8,128)S(1)} custom-call(f32[640]{0:T(1024)} %rate_hbm.1, s32[2,8]{1,0:T(2,128)} %reset_hbm.1, bf16[1280,128]{1,0:T(8,128)(2,1)} %bitcast.23, bf16[1280,128]{1,0:T(8,128)(2,1)} %bitcast.24, bf16[1280,128]{1,0:T(8,128)(2,1)} %bitcast.25), custom_call_target="tpu_custom_call" | custom-call | tf_op jit(solution)/shard_map/scan/pallas_call | solution.py:257
  4.8 26.9 %all_to_all.10 = s32[32,22,1,128]{3,2,1,0:T(1,128)S(1)} all-to-all(s32[32,22,1,128]{3,2,1,0:T(1,128)S(1)} %bitcast.21), channel_id=1, replica_groups=mesh['seq_0'=8,'seq_1'=4,'seq_2'=2,'chan'=8] {'seq_0','seq_1'}, dimensions={0} | all-to-all | bytes 720896 | tf_op jit(solution)/shard_map/all_to_all | solution.py:283
  31.6 4.1 %collective-permute-start = (s32[704,128]{1,0:T(8,128)S(1)}, s32[704,128]{1,0:T(8,128)S(1)}, u32[]{:S(2)}, u32[]{:S(2)}) collective-permute-start(s32[704,128]{1,0:T(8,128)S(1)} %bitcast.18), channel_id=1, source_target_pairs={{0,8},{8,0},{1,9},{9,1},{2,10},{10,2},{3,11},{11,3},{4,12},{12,4},... | collective-permute-start | bytes 1081352 | tf_op jit(solution)/shard_map/ppermute | solution.py:294
  35.7 0.7 %squares.1 = f32[16,2,128]{2,1,0:T(2,128)} custom-call(s32[704,128]{1,0:T(8,128)S(1)} %bitcast.19), custom_call_target="tpu_custom_call" | custom-call | tf_op jit(solution)/shard_map/squares/pallas_call | solution.py:285
  36.5 0.0 copy-start
  36.5 7.4 %all-to-all-start.1 = ((f32[16,2,128]{2,1,0:T(2,128)}), f32[16,2,128]{2,1,0:T(2,128)S(1)}, u32[]{:S(2)}, u32[]{:S(2)}) async-start(f32[16,2,128]{2,1,0:T(2,128)} %squares.1), calls=%async_computation.1 | async-start | bytes 32768 | tf_op jit(solution)/shard_map/all_to_all | solution.py:293
  43.9 0.0 copy-done
  43.9 0.2 gain.1.gain_ref
  44.0 6.8 %all-to-all-done.1.sum_ref = f32[16,2,128]{2,1,0:T(2,128)S(1)} async-done(((f32[16,2,128]{2,1,0:T(2,128)}), f32[16,2,128]{2,1,0:T(2,128)S(1)}, u32[]{:S(2)}, u32[]{:S(2)}) %all-to-all-start.1) | async-done | bytes 16416 | tf_op jit(solution)/shard_map/all_to_all | solution.py:293
  50.9 0.0 collective-permute-done.mate_ref
  50.9 0.9 %final.1 = bf16[2,640,128]{2,1,0:T(8,128)(2,1)} custom-call(s32[704,128]{1,0:T(8,128)S(1)} %bitcast.20, s32[704,128]{1,0:T(8,128)S(1)} %collective-permute-done.mate_ref, f32[16,2,128]{2,1,0:T(2,128)S(1)} %all-to-all-done.1.sum_ref, f32[640,128]{1,0:T(8,128)S(1)} %gain.1.gain_ref), custom_call_target="tpu_custom_call" | custom-call | tf_op jit(solution)/shard_map/final/pallas_call | solution.py:304
Async XLA Ops:
  31.6 19.2 %collective-permute-start = (s32[704,128]{1,0:T(8,128)S(1)}, s32[704,128]{1,0:T(8,128)S(1)}, u32[]{:S(2)}, u32[]{:S(2)}) collective-permute-start(s32[704,128]{1,0:T(8,128)S(1)} %bitcast.18), channel_id=1, source_target_pairs={{0,8},{8,0},{1,9},{9,1},{2,10},{10,2},{3,11},{11,3},{4,12},{12,4},... | collective-permute-start | bytes 1081352 | tf_op jit(solution)/shard_map/ppermute | solution.py:294
  36.5 7.4 %copy-start = (f32[640]{0:T(1024)S(1)}, f32[640]{0:T(1024)}, u32[]{:S(2)}) copy-start(f32[640]{0:T(1024)} %param.10) | copy-start | bytes 7684
  36.5 14.4 %all-to-all-start.1 = ((f32[16,2,128]{2,1,0:T(2,128)}), f32[16,2,128]{2,1,0:T(2,128)S(1)}, u32[]{:S(2)}, u32[]{:S(2)}) async-start(f32[16,2,128]{2,1,0:T(2,128)} %squares.1), calls=%async_computation.1 | async-start | bytes 32768 | tf_op jit(solution)/shard_map/all_to_all | solution.py:293

commit v4 on v3

--- a/solution.py
+++ b/solution.py
@@ -20,7 +20,7 @@
 CODE_ZERO = 16384.0
 CORES = 2
 LOG2E = 1.4426950408889634
-UNROLL = 2
+GROUP = 5
 
 
 def root_of_one_minus_exp(x, expo):
@@ -66,7 +66,7 @@
     sources = ((step_hbm, step_ref), (inp_hbm, inp_ref), (gate_hbm, gate_ref))
 
     def fetch(k, c):
-        at = pl.ds(pl.multiple_of(c * count, count), count)
+        at = pl.ds(c * count, count)
         return pltpu.make_async_copy(sources[k][0].at[at], sources[k][1].at[at], sems.at[k, c])
 
     scalars = [
@@ -90,13 +90,11 @@
         for mark in marks[1:]:
             hit = hit | (t == mark)
         live[tile(v), :] = jnp.where(hit, 0.0, 1.0)
-        top[tile(v), :] = jnp.full((SUB, LANES), 1e-37, jnp.float32)
+        top[tile(v), :] = jnp.full((SUB, LANES), 1e-30, jnp.float32)
     tot[...] = jnp.zeros_like(tot)
 
-    def local(c, _):
-        at = pl.ds(pl.multiple_of(c * count, count), count)
-        fetch(0, c).wait()
-        fetch(1, c).wait()
+    def local(c):
+        at = tile_of(c, count)
         scaled = step_ref[at, :].astype(jnp.float32) * rate_ref[place * width + c]
         expo = jnp.exp2(scaled * (-LOG2E))
         drive = root_of_one_minus_exp(scaled + scaled, expo) * inp_ref[at, :].astype(jnp.float32)
@@ -112,38 +110,60 @@
             if v:
                 s = s + a * end_s
                 a = a * end_a
-            here = pl.ds(pl.multiple_of(c * count + v * SUB, SUB), SUB)
+            here = tile(c * tiles + v)
             held[0, here, :] = a
             held[1, here, :] = s
             end_a = jnp.broadcast_to(a[SUB - 1 :], (SUB, LANES))
             end_s = jnp.broadcast_to(s[SUB - 1 :], (SUB, LANES))
-        tot[0, pl.ds(c, 1), :] = end_a[:1]
-        tot[1, pl.ds(c, 1), :] = end_s[:1]
-        return 0
-
-    lax.fori_loop(0, width, local, 0, unroll=UNROLL)
+        tot[0, c : c + 1, :] = end_a[:1]
+        tot[1, c : c + 1, :] = end_s[:1]
+
+    for low in range(0, width, GROUP):
+        group = range(low, min(width, low + GROUP))
+        for c in group:
+            fetch(0, c).wait()
+            fetch(1, c).wait()
+        for c in group:
+            local(c)
+    for c in range(width):
+        fetch(2, c).wait()
 
     wide = lax.broadcasted_iota(jnp.int32, tot.shape[1:], 1)
     a, s = tot[0], tot[1]
-    k = batch
-    while k < count:
-        keep = wide >= k
-        s = s + a * jnp.where(keep, pltpu.roll(s, k, 1), 0.0)
-        a = a * jnp.where(keep, pltpu.roll(a, k, 1), 1.0)
-        k *= 2
-    tot[0] = jnp.where(wide >= batch, pltpu.roll(s, batch, 1), 0.0)
-
-    def emit(c, _):
-        at = pl.ds(pl.multiple_of(c * count, count), count)
-        state = (held[1, at, :] + held[0, at, :] * tot[0, pl.ds(c, 1), :]).T
-        fetch(2, c).wait()
+    span, offset = batch, batch
+    while span < count:
+        terms = []
+        for k in range(4):
+            shift = offset + k * span
+            if shift >= count:
+                break
+            if not shift:
+                terms.append((a, s))
+                continue
+            keep = wide >= shift
+            terms.append(
+                (
+                    jnp.where(keep, pltpu.roll(a, shift, 1), 1.0),
+                    jnp.where(keep, pltpu.roll(s, shift, 1), 0.0),
+                )
+            )
+        a, s = terms[-1]
+        for later_a, later_s in terms[-2::-1]:
+            s = later_s + later_a * s
+            a = later_a * a
+        span, offset = span * 4, 0
+    tot[0] = s
+
+    def emit(c):
+        at = tile_of(c, count)
+        state = (held[1, at, :] + held[0, at, :] * tot[0, c : c + 1, :]).T
         g = gate_ref[at, :].astype(jnp.float32)
         value = state * (g / (1.0 + jnp.exp2(g * (-LOG2E))))
         held[2, at, :] = value
         top[...] = jnp.maximum(top[...], jnp.abs(value))
-        return 0
-
-    lax.fori_loop(0, width, emit, 0, unroll=UNROLL)
+
+    for c in range(width):
+        emit(c)
 
     e = jnp.ceil(jnp.log2(top[...]) * FINE)
     top[...] = jnp.exp2(e * (-1.0 / FINE)) * LEVELS

time: 52.1 us -> 50.4 us (0.967)
  Pallas kernels: 6.58 us -> 4.89 us
    pallas_call x1, Pallas kernels: 4.75 us -> 3.06 us  [per_device(): pl.pallas_call(functools.partial(scan_kernel, (batch, width, blocks, rese...]
where the time goes in v4:
time: 50.4 us; the launch traced here: 50.1 us
  blocking collectives  26.9 us (53%)
  starting transfers between devices  11.5 us (23%)
  waiting for transfers between devices  6.85 us (14%)
  Pallas kernels  4.89 us (10%)
    all_to_all x1, blocking collectives, per_device(): words = lax.all_to_all(words, ('seq_0', 'seq_1'), 0, 0, tiled=True)  26.9 us
    all_to_all x1, starting transfers between devices, per_device(): sums = lax.all_to_all(sums, ('seq_2', 'chan'), 0, 0, tiled=True)  7.36 us
    all_to_all x1, waiting for transfers between devices, per_device(): sums = lax.all_to_all(sums, ('seq_2', 'chan'), 0, 0, tiled=True)  6.84 us
    ppermute x1, starting transfers between devices, per_device(): mate = lax.ppermute(words, 'seq_2', [(0, 1), (1, 0)])  4.11 us
    pallas_call x1, Pallas kernels, per_device(): pl.pallas_call(functools.partial(scan_kernel, (batch, width, blocks, rese...  3.06 us
  transfers between devices with their start and end apart: 2, of which 1 were waited for; matrix products, arithmetic and copies ran while one was open for 0% of the time, Pallas kernels for 2%

profile of v4, /device:TPU:1, one launch (start us, length us, event | category | flops | bytes accessed | tf_op | source)
XLA Modules:
  0.0 50.1 jit_solution(10568155368072096372)
XLA Ops:
  0.0 3.1 %scan.1 = s32[704,128]{1,0:T(8,128)S(1)} custom-call(f32[640]{0:T(1024)} %rate_hbm.1, s32[2,8]{1,0:T(2,128)} %reset_hbm.1, bf16[1280,128]{1,0:T(8,128)(2,1)} %bitcast.23, bf16[1280,128]{1,0:T(8,128)(2,1)} %bitcast.24, bf16[1280,128]{1,0:T(8,128)(2,1)} %bitcast.25), custom_call_target="tpu_custom_call" | custom-call | tf_op jit(solution)/shard_map/scan/pallas_call | solution.py:277
  3.1 26.9 %all_to_all.10 = s32[32,22,1,128]{3,2,1,0:T(1,128)S(1)} all-to-all(s32[32,22,1,128]{3,2,1,0:T(1,128)S(1)} %bitcast.21), channel_id=1, replica_groups=mesh['seq_0'=8,'seq_1'=4,'seq_2'=2,'chan'=8] {'seq_0','seq_1'}, dimensions={0} | all-to-all | bytes 720896 | tf_op jit(solution)/shard_map/all_to_all | solution.py:303
  29.9 4.1 %collective-permute-start = (s32[704,128]{1,0:T(8,128)S(1)}, s32[704,128]{1,0:T(8,128)S(1)}, u32[]{:S(2)}, u32[]{:S(2)}) collective-permute-start(s32[704,128]{1,0:T(8,128)S(1)} %bitcast.18), channel_id=1, source_target_pairs={{0,8},{8,0},{1,9},{9,1},{2,10},{10,2},{3,11},{11,3},{4,12},{12,4},... | collective-permute-start | bytes 1081352 | tf_op jit(solution)/shard_map/ppermute | solution.py:314
  34.1 0.7 %squares.1 = f32[16,2,128]{2,1,0:T(2,128)} custom-call(s32[704,128]{1,0:T(8,128)S(1)} %bitcast.19), custom_call_target="tpu_custom_call" | custom-call | tf_op jit(solution)/shard_map/squares/pallas_call | solution.py:305
  34.8 0.0 copy-start
  34.8 7.4 %all-to-all-start.1 = ((f32[16,2,128]{2,1,0:T(2,128)}), f32[16,2,128]{2,1,0:T(2,128)S(1)}, u32[]{:S(2)}, u32[]{:S(2)}) async-start(f32[16,2,128]{2,1,0:T(2,128)} %squares.1), calls=%async_computation.1 | async-start | bytes 32768 | tf_op jit(solution)/shard_map/all_to_all | solution.py:313
  42.2 0.0 copy-done
  42.2 0.2 gain.1.gain_ref
  42.3 6.8 %all-to-all-done.1.sum_ref = f32[16,2,128]{2,1,0:T(2,128)S(1)} async-done(((f32[16,2,128]{2,1,0:T(2,128)}), f32[16,2,128]{2,1,0:T(2,128)S(1)}, u32[]{:S(2)}, u32[]{:S(2)}) %all-to-all-start.1) | async-done | bytes 16416 | tf_op jit(solution)/shard_map/all_to_all | solution.py:313
  49.2 0.0 collective-permute-done.mate_ref
  49.2 0.9 %final.1 = bf16[2,640,128]{2,1,0:T(8,128)(2,1)} custom-call(s32[704,128]{1,0:T(8,128)S(1)} %bitcast.20, s32[704,128]{1,0:T(8,128)S(1)} %collective-permute-done.mate_ref, f32[16,2,128]{2,1,0:T(2,128)S(1)} %all-to-all-done.1.sum_ref, f32[640,128]{1,0:T(8,128)S(1)} %gain.1.gain_ref), custom_call_target="tpu_custom_call" | custom-call | tf_op jit(solution)/shard_map/final/pallas_call | solution.py:324
Async XLA Ops:
  29.9 19.2 %collective-permute-start = (s32[704,128]{1,0:T(8,128)S(1)}, s32[704,128]{1,0:T(8,128)S(1)}, u32[]{:S(2)}, u32[]{:S(2)}) collective-permute-start(s32[704,128]{1,0:T(8,128)S(1)} %bitcast.18), channel_id=1, source_target_pairs={{0,8},{8,0},{1,9},{9,1},{2,10},{10,2},{3,11},{11,3},{4,12},{12,4},... | collective-permute-start | bytes 1081352 | tf_op jit(solution)/shard_map/ppermute | solution.py:314
  34.8 7.4 %copy-start = (f32[640]{0:T(1024)S(1)}, f32[640]{0:T(1024)}, u32[]{:S(2)}) copy-start(f32[640]{0:T(1024)} %param.10) | copy-start | bytes 7684
  34.8 14.4 %all-to-all-start.1 = ((f32[16,2,128]{2,1,0:T(2,128)}), f32[16,2,128]{2,1,0:T(2,128)S(1)}, u32[]{:S(2)}, u32[]{:S(2)}) async-start(f32[16,2,128]{2,1,0:T(2,128)} %squares.1), calls=%async_computation.1 | async-start | bytes 32768 | tf_op jit(solution)/shard_map/all_to_all | solution.py:313

commit v5 on v4

--- a/solution.py
+++ b/solution.py
@@ -21,6 +21,10 @@
 CORES = 2
 LOG2E = 1.4426950408889634
 GROUP = 5
+TURN = 6
+SIDE = 2
+HEAD_CORE = 1
+HEAD_CHAN = 5
 
 
 def root_of_one_minus_exp(x, expo):
@@ -177,7 +181,9 @@
         for m in range(blocks // SUB):
             base = c * count + m * SUB * batch
             first, second = [ints[pl.ds(base + b, SUB, stride=batch), :] for b in range(batch)]
-            out_ref[pl.ds(m * SUB * record + c, SUB, stride=record), :] = first * 65536 | second
+            to = (m - TURN) % (blocks // SUB) * SUB * record + c
+            word = pltpu.roll(first * 65536 | second, SUB - SIDE * CORES, 0)
+            out_ref[pl.ds(to, SUB, stride=record), :] = word
 
 
 def tile_of(c, count):
@@ -218,7 +224,12 @@
         for b in range(2):
             row = jnp.sum(acc[b], axis=0, keepdims=True)
             for y in range(chan):
-                sum_ref[k * chan + y, b : b + 1, :] = row
+                sum_ref[(k - HEAD_CORE) % CORES * chan + y, b : b + 1, :] = row
+
+
+def straight(word):
+    sub = lax.broadcasted_iota(jnp.int32, (SUB, LANES), 0)
+    return jnp.where((sub & 2) == 0, pltpu.roll(word, SUB - SIDE, 0), pltpu.roll(word, SIDE, 0))
 
 
 def gain_kernel(gain_ref, out_ref):
@@ -240,14 +251,14 @@
         def words(c):
             a = words_at(own_ref, m, mine, c, record)
             b = words_at(mate_ref, m, mine, c, record)
-            return jnp.where(mine == 0, a, b), jnp.where(mine == 0, b, a)
+            return straight(jnp.where(mine == 0, a, b)), straight(jnp.where(mine == 0, b, a))
 
         scale = [scales(w) for w in words(width)]
         scale = [[s * norm[b : b + 1] for b, s in enumerate(pair)] for pair in scale]
         for c in range(width):
             for k, word in enumerate(words(c)):
                 for b, q in enumerate(opened(word)):
-                    row = (m * SUB * CORES + k) * width + c
+                    row = ((m + TURN // 2) % (chips // SUB) * SUB * CORES + k) * width + c
                     flat[b, pl.ds(row, SUB, stride=CORES * width), :] = (q - MIDDLE) * scale[k][b]
     for b in range(2):
         out_ref[b] = (flat[b] * gain_ref[...]).astype(jnp.bfloat16)
@@ -300,7 +311,13 @@
         ],
     )
     words = words.reshape(chips, cores * record, 1, LANES)
-    words = lax.all_to_all(words, ("seq_0", "seq_1"), 0, 0, tiled=True)
+    deep, side = lax.axis_size("seq_0"), lax.axis_size("seq_1")
+    turned = [
+        [(z + TURN) % deep * side + (x + SIDE) % side for z in range(deep) for x in range(side)]
+    ]
+    words = lax.all_to_all(
+        words, ("seq_0", "seq_1"), 0, 0, axis_index_groups=turned, tiled=True
+    )
     words = words.reshape(blocks * record, LANES)
     sums = pl.pallas_call(
         functools.partial(squares_kernel, (width, chips)),
@@ -310,7 +327,16 @@
         compiler_params=room(8),
         name="squares",
     )(words)
-    sums = lax.all_to_all(sums, ("seq_2", "chan"), 0, 0, tiled=True)
+    order = [
+        [
+            (k + HEAD_CORE) % cores * chan + (y + HEAD_CHAN) % chan
+            for k in range(cores)
+            for y in range(chan)
+        ]
+    ]
+    sums = lax.all_to_all(
+        sums, ("seq_2", "chan"), 0, 0, axis_index_groups=order, tiled=True
+    )
     mate = lax.ppermute(words, "seq_2", [(0, 1), (1, 0)])
     channels = blocks * width
     gain = pl.pallas_call(

time: 50.4 us -> 44.8 us (0.89)
  waiting for transfers between devices: 6.85 us -> 3.17 us
  blocking collectives: 26.9 us -> 23.7 us
  starting transfers between devices: 11.5 us -> 12.6 us
    all_to_all x1, waiting for transfers between devices: 6.84 us -> 3.17 us  [per_device(): lax.all_to_all(sums, ('seq_2', 'chan'), 0, 0, axis_index_groups=order, ti...]
    all_to_all x1, blocking collectives: 26.9 us -> 23.7 us  [per_device(): lax.all_to_all(words, ('seq_0', 'seq_1'), 0, 0, axis_index_groups=turned,...]
    all_to_all x1, starting transfers between devices: 7.36 us -> 8.19 us  [per_device(): lax.all_to_all(sums, ('seq_2', 'chan'), 0, 0, axis_index_groups=order, ti...]
where the time goes in v5:
time: 44.8 us; the launch traced here: 44.5 us
  blocking collectives  23.7 us (53%)
  starting transfers between devices  12.6 us (28%)
  Pallas kernels  4.95 us (11%)
  waiting for transfers between devices  3.17 us (7%)
    all_to_all x1, blocking collectives, per_device(): lax.all_to_all(words, ('seq_0', 'seq_1'), 0, 0, axis_index_groups=turned,...  23.7 us
    all_to_all x1, starting transfers between devices, per_device(): lax.all_to_all(sums, ('seq_2', 'chan'), 0, 0, axis_index_groups=order, ti...  8.19 us
    ppermute x1, starting transfers between devices, per_device(): mate = lax.ppermute(words, 'seq_2', [(0, 1), (1, 0)])  4.37 us
    all_to_all x1, waiting for transfers between devices, per_device(): lax.all_to_all(sums, ('seq_2', 'chan'), 0, 0, axis_index_groups=order, ti...  3.17 us
    pallas_call x1, Pallas kernels, per_device(): pl.pallas_call(functools.partial(scan_kernel, (batch, width, blocks, rese...  3.08 us
    pallas_call x1, Pallas kernels, per_device(): pl.pallas_call(functools.partial(final_kernel, (width, chips)), out_shape...  0.97 us
  transfers between devices with their start and end apart: 2, of which 1 were waited for; matrix products, arithmetic and copies ran while one was open for 0% of the time, Pallas kernels for 2%

profile of v5, /device:TPU:1, one launch (start us, length us, event | category | flops | bytes accessed | tf_op | source)
XLA Modules:
  0.0 44.5 jit_solution(11708012586167598457)
XLA Ops:
  0.0 3.1 %scan.1 = s32[704,128]{1,0:T(8,128)S(1)} custom-call(f32[640]{0:T(1024)} %rate_hbm.1, s32[2,8]{1,0:T(2,128)} %reset_hbm.1, bf16[1280,128]{1,0:T(8,128)(2,1)} %bitcast.23, bf16[1280,128]{1,0:T(8,128)(2,1)} %bitcast.24, bf16[1280,128]{1,0:T(8,128)(2,1)} %bitcast.25), custom_call_target="tpu_custom_call" | custom-call | tf_op jit(solution)/shard_map/scan/pallas_call | solution.py:288
  3.1 23.7 %all_to_all.10 = s32[32,22,1,128]{3,2,1,0:T(1,128)S(1)} all-to-all(s32[32,22,1,128]{3,2,1,0:T(1,128)S(1)} %bitcast.21), channel_id=1, replica_groups={{416,432,384,400,480,496,448,464,32,48,0,16,96,112,64,80,160,176,128,14..., dimensions={0} | all-to-all | bytes 720896 | tf_op jit(solution)/shard_map/all_to_all | solution.py:318
  26.8 4.4 %collective-permute-start = (s32[704,128]{1,0:T(8,128)S(1)}, s32[704,128]{1,0:T(8,128)S(1)}, u32[]{:S(2)}, u32[]{:S(2)}) collective-permute-start(s32[704,128]{1,0:T(8,128)S(1)} %bitcast.18), channel_id=1, source_target_pairs={{0,8},{8,0},{1,9},{9,1},{2,10},{10,2},{3,11},{11,3},{4,12},{12,4},... | collective-permute-start | bytes 1081352 | tf_op jit(solution)/shard_map/ppermute | solution.py:340
  31.2 0.7 %squares.1 = f32[16,2,128]{2,1,0:T(2,128)} custom-call(s32[704,128]{1,0:T(8,128)S(1)} %bitcast.19), custom_call_target="tpu_custom_call" | custom-call | tf_op jit(solution)/shard_map/squares/pallas_call | solution.py:322
  32.0 0.0 copy-start
  32.0 8.2 %all-to-all-start.1 = ((f32[16,2,128]{2,1,0:T(2,128)}), f32[16,2,128]{2,1,0:T(2,128)S(1)}, u32[]{:S(2)}, u32[]{:S(2)}) async-start(f32[16,2,128]{2,1,0:T(2,128)} %squares.1), calls=%async_computation.1 | async-start | bytes 32768 | tf_op jit(solution)/shard_map/all_to_all | solution.py:337
  40.1 0.0 copy-done
  40.1 0.2 gain.1.gain_ref
  40.3 3.2 %all-to-all-done.1.sum_ref = f32[16,2,128]{2,1,0:T(2,128)S(1)} async-done(((f32[16,2,128]{2,1,0:T(2,128)}), f32[16,2,128]{2,1,0:T(2,128)S(1)}, u32[]{:S(2)}, u32[]{:S(2)}) %all-to-all-start.1) | async-done | bytes 16416 | tf_op jit(solution)/shard_map/all_to_all | solution.py:337
  43.5 0.0 collective-permute-done.mate_ref
  43.5 1.0 %final.1 = bf16[2,640,128]{2,1,0:T(8,128)(2,1)} custom-call(s32[704,128]{1,0:T(8,128)S(1)} %bitcast.20, s32[704,128]{1,0:T(8,128)S(1)} %collective-permute-done.mate_ref, f32[16,2,128]{2,1,0:T(2,128)S(1)} %all-to-all-done.1.sum_ref, f32[640,128]{1,0:T(8,128)S(1)} %gain.1.gain_ref), custom_call_target="tpu_custom_call" | custom-call | tf_op jit(solution)/shard_map/final/pallas_call | solution.py:350
Async XLA Ops:
  26.8 16.7 %collective-permute-start = (s32[704,128]{1,0:T(8,128)S(1)}, s32[704,128]{1,0:T(8,128)S(1)}, u32[]{:S(2)}, u32[]{:S(2)}) collective-permute-start(s32[704,128]{1,0:T(8,128)S(1)} %bitcast.18), channel_id=1, source_target_pairs={{0,8},{8,0},{1,9},{9,1},{2,10},{10,2},{3,11},{11,3},{4,12},{12,4},... | collective-permute-start | bytes 1081352 | tf_op jit(solution)/shard_map/ppermute | solution.py:340
  32.0 8.2 %copy-start = (f32[640]{0:T(1024)S(1)}, f32[640]{0:T(1024)}, u32[]{:S(2)}) copy-start(f32[640]{0:T(1024)} %param.10) | copy-start | bytes 7684
  32.0 11.5 %all-to-all-start.1 = ((f32[16,2,128]{2,1,0:T(2,128)}), f32[16,2,128]{2,1,0:T(2,128)S(1)}, u32[]{:S(2)}, u32[]{:S(2)}) async-start(f32[16,2,128]{2,1,0:T(2,128)} %squares.1), calls=%async_computation.1 | async-start | bytes 32768 | tf_op jit(solution)/shard_map/all_to_all | solution.py:337

commit v6 on v5

--- a/solution.py
+++ b/solution.py
@@ -20,7 +20,7 @@
 CODE_ZERO = 16384.0
 CORES = 2
 LOG2E = 1.4426950408889634
-GROUP = 5
+EDGES = (0, 2, 10)
 TURN = 6
 SIDE = 2
 HEAD_CORE = 1
@@ -122,8 +122,8 @@
         tot[0, c : c + 1, :] = end_a[:1]
         tot[1, c : c + 1, :] = end_s[:1]
 
-    for low in range(0, width, GROUP):
-        group = range(low, min(width, low + GROUP))
+    for low, high in zip(EDGES, (*EDGES[1:], width)):
+        group = range(min(low, width), min(high, width))
         for c in group:
             fetch(0, c).wait()
             fetch(1, c).wait()
@@ -238,7 +238,7 @@
         out_ref[g * LANES : (g + 1) * LANES, :] = jnp.broadcast_to(row, (LANES, LANES)).T
 
 
-def final_kernel(sizes, own_ref, mate_ref, sum_ref, gain_ref, out_ref, flat):
+def final_kernel(sizes, own_ref, mate_ref, sum_ref, gain_ref, out_hbm, flat, out_ref, sems):
     width, chips = sizes
     mine = lax.axis_index("seq_2")
     record = width + 1
@@ -260,8 +260,13 @@
                 for b, q in enumerate(opened(word)):
                     row = ((m + TURN // 2) % (chips // SUB) * SUB * CORES + k) * width + c
                     flat[b, pl.ds(row, SUB, stride=CORES * width), :] = (q - MIDDLE) * scale[k][b]
+    copies = []
     for b in range(2):
         out_ref[b] = (flat[b] * gain_ref[...]).astype(jnp.bfloat16)
+        copies.append(pltpu.make_async_copy(out_ref.at[b], out_hbm.at[b], sems.at[b]))
+        copies[-1].start()
+    for copy in copies:
+        copy.wait()
 
 
 def whole(space=pltpu.VMEM):
@@ -351,8 +356,12 @@
         functools.partial(final_kernel, (width, chips)),
         out_shape=jax.ShapeDtypeStruct((batch, channels, LANES), jnp.bfloat16),
         in_specs=[whole()] * 4,
-        out_specs=whole(),
-        scratch_shapes=[pltpu.VMEM((batch, channels, LANES), jnp.float32)],
+        out_specs=whole(pltpu.HBM),
+        scratch_shapes=[
+            pltpu.VMEM((batch, channels, LANES), jnp.float32),
+            pltpu.VMEM((batch, channels, LANES), jnp.bfloat16),
+            pltpu.SemaphoreType.DMA((2,)),
+        ],
         compiler_params=room(8),
         name="final",
     )(words, mate, sums, gain)

time: 44.8 us -> 44.8 us (level)
  no operation moved by 1% of the time
where the time goes in v6:
time: 44.8 us; the launch traced here: 44.5 us
  blocking collectives  23.7 us (53%)
  starting transfers between devices  12.6 us (28%)
  Pallas kernels  4.99 us (11%)
  waiting for transfers between devices  3.17 us (7%)
    all_to_all x1, blocking collectives, per_device(): lax.all_to_all(words, ('seq_0', 'seq_1'), 0, 0, axis_index_groups=turned,...  23.7 us
    all_to_all x1, starting transfers between devices, per_device(): lax.all_to_all(sums, ('seq_2', 'chan'), 0, 0, axis_index_groups=order, ti...  8.19 us
    ppermute x1, starting transfers between devices, per_device(): mate = lax.ppermute(words, 'seq_2', [(0, 1), (1, 0)])  4.37 us
    all_to_all x1, waiting for transfers between devices, per_device(): lax.all_to_all(sums, ('seq_2', 'chan'), 0, 0, axis_index_groups=order, ti...  3.17 us
    pallas_call x1, Pallas kernels, per_device(): pl.pallas_call(functools.partial(scan_kernel, (batch, width, blocks, rese...  3.15 us
    pallas_call x1, Pallas kernels, per_device(): pl.pallas_call(functools.partial(final_kernel, (width, chips)), out_shape...  0.94 us
  transfers between devices with their start and end apart: 2, of which 1 were waited for; matrix products, arithmetic and copies ran while one was open for 0% of the time, Pallas kernels for 2%

profile of v6, /device:TPU:1, one launch (start us, length us, event | category | flops | bytes accessed | tf_op | source)
XLA Modules:
  0.0 44.5 jit_solution(3082541473566785400)
XLA Ops:
  0.0 3.1 %scan.1 = s32[704,128]{1,0:T(8,128)S(1)} custom-call(f32[640]{0:T(1024)} %rate_hbm.1, s32[2,8]{1,0:T(2,128)} %reset_hbm.1, bf16[1280,128]{1,0:T(8,128)(2,1)} %bitcast.23, bf16[1280,128]{1,0:T(8,128)(2,1)} %bitcast.24, bf16[1280,128]{1,0:T(8,128)(2,1)} %bitcast.25), custom_call_target="tpu_custom_call" | custom-call | tf_op jit(solution)/shard_map/scan/pallas_call | solution.py:293
  3.2 23.7 %all_to_all.10 = s32[32,22,1,128]{3,2,1,0:T(1,128)S(1)} all-to-all(s32[32,22,1,128]{3,2,1,0:T(1,128)S(1)} %bitcast.21), channel_id=1, replica_groups={{416,432,384,400,480,496,448,464,32,48,0,16,96,112,64,80,160,176,128,14..., dimensions={0} | all-to-all | bytes 720896 | tf_op jit(solution)/shard_map/all_to_all | solution.py:323
  26.9 4.4 %collective-permute-start = (s32[704,128]{1,0:T(8,128)S(1)}, s32[704,128]{1,0:T(8,128)S(1)}, u32[]{:S(2)}, u32[]{:S(2)}) collective-permute-start(s32[704,128]{1,0:T(8,128)S(1)} %bitcast.18), channel_id=1, source_target_pairs={{0,8},{8,0},{1,9},{9,1},{2,10},{10,2},{3,11},{11,3},{4,12},{12,4},... | collective-permute-start | bytes 1081352 | tf_op jit(solution)/shard_map/ppermute | solution.py:345
  31.3 0.7 %squares.1 = f32[16,2,128]{2,1,0:T(2,128)} custom-call(s32[704,128]{1,0:T(8,128)S(1)} %bitcast.19), custom_call_target="tpu_custom_call" | custom-call | tf_op jit(solution)/shard_map/squares/pallas_call | solution.py:327
  32.0 0.0 copy-start
  32.0 8.2 %all-to-all-start.1 = ((f32[16,2,128]{2,1,0:T(2,128)}), f32[16,2,128]{2,1,0:T(2,128)S(1)}, u32[]{:S(2)}, u32[]{:S(2)}) async-start(f32[16,2,128]{2,1,0:T(2,128)} %squares.1), calls=%async_computation.1 | async-start | bytes 32768 | tf_op jit(solution)/shard_map/all_to_all | solution.py:342
  40.2 0.0 copy-done
  40.2 0.2 gain.1.gain_ref
  40.4 3.2 %all-to-all-done.1.sum_ref = f32[16,2,128]{2,1,0:T(2,128)S(1)} async-done(((f32[16,2,128]{2,1,0:T(2,128)}), f32[16,2,128]{2,1,0:T(2,128)S(1)}, u32[]{:S(2)}, u32[]{:S(2)}) %all-to-all-start.1) | async-done | bytes 16416 | tf_op jit(solution)/shard_map/all_to_all | solution.py:342
  43.5 0.0 collective-permute-done.mate_ref
  43.5 0.9 %final.1 = bf16[2,640,128]{2,1,0:T(8,128)(2,1)} custom-call(s32[704,128]{1,0:T(8,128)S(1)} %bitcast.20, s32[704,128]{1,0:T(8,128)S(1)} %collective-permute-done.mate_ref, f32[16,2,128]{2,1,0:T(2,128)S(1)} %all-to-all-done.1.sum_ref, f32[640,128]{1,0:T(8,128)S(1)} %gain.1.gain_ref), custom_call_target="tpu_custom_call" | custom-call | tf_op jit(solution)/shard_map/final/pallas_call | solution.py:355
Async XLA Ops:
  26.9 16.7 %collective-permute-start = (s32[704,128]{1,0:T(8,128)S(1)}, s32[704,128]{1,0:T(8,128)S(1)}, u32[]{:S(2)}, u32[]{:S(2)}) collective-permute-start(s32[704,128]{1,0:T(8,128)S(1)} %bitcast.18), channel_id=1, source_target_pairs={{0,8},{8,0},{1,9},{9,1},{2,10},{10,2},{3,11},{11,3},{4,12},{12,4},... | collective-permute-start | bytes 1081352 | tf_op jit(solution)/shard_map/ppermute | solution.py:345
  32.0 8.2 %copy-start = (f32[640]{0:T(1024)S(1)}, f32[640]{0:T(1024)}, u32[]{:S(2)}) copy-start(f32[640]{0:T(1024)} %param.10) | copy-start | bytes 7684
  32.0 11.5 %all-to-all-start.1 = ((f32[16,2,128]{2,1,0:T(2,128)}), f32[16,2,128]{2,1,0:T(2,128)S(1)}, u32[]{:S(2)}, u32[]{:S(2)}) async-start(f32[16,2,128]{2,1,0:T(2,128)} %squares.1), calls=%async_computation.1 | async-start | bytes 32768 | tf_op jit(solution)/shard_map/all_to_all | solution.py:342
